TPU v7x, 256 devices: a whole 4x4x8 slice. The times are simulated.
256 devices in a mesh: expert: 32 (over x, z_lo, y), dp: 8 (over z_hi, core).
Axes of the slice: x: 4, y: 4, z: 8 (z_hi: 4, z_lo: 2; z = z_hi * 2 + z_lo), core: 2. Of those that a mesh axis runs over, the one named last changes fastest.
Arguments:
- tokens: bfloat16 [32768, 1440], P(('expert', 'dp')), may hold values from -6 to 6
- cotangent: bfloat16 [32768, 1440], P(('expert', 'dp')), may hold values from -0.3984375 to 0.3984375
- expert_ids: int32 [32768, 4], P(('expert', 'dp')), may hold values from 0 to 31, all different within a row; in each aligned block of 128 rows (0 to 127, 128 to 255, ...) at most 24 rows name the same one
- gate_weights: float32 [32768, 4], P(('expert', 'dp')), may hold values from 0.05 to 1
- w_gate: bfloat16 [32, 1440, 1440], P('expert', 'dp'), may hold values from -0.15625 to 0.15625
- w_up: bfloat16 [32, 1440, 1440], P('expert', 'dp'), may hold values from -0.15625 to 0.15625
- w_down: bfloat16 [32, 1440, 1440], P('expert', 'dp'), may hold values from -0.15625 to 0.15625
Outputs:
- mixed: bfloat16 [32768, 1440], P(('expert', 'dp'))
- grad_gate: bfloat16 [32, 1440, 1440], P('expert', 'dp')
- grad_up: bfloat16 [32, 1440, 1440], P('expert', 'dp')
- grad_down: bfloat16 [32, 1440, 1440], P('expert', 'dp')
Inputs may be any that keep to these rules, and one draw needn't show every extreme that they name: `expert_ids`: each row names 4 different experts. Within the rows of one device no expert is named more than 24 times, a bound that some block reaches.
All inputs are finite; a program needn't handle non-finite values.
Results may differ from a plain program's by a relative error of at most 0.013.
Values may be sent and summed in bfloat16 or wider, within the bound.
A program may use at most 128 MiB of HBM per device.

v0:
```python
import jax
import jax.numpy as jnp
from jax import lax
from jax.sharding import PartitionSpec as P

CAP = 512


SWISH_SLOPE = 1.702


def copy_for_each(value, axis):
    copies = jnp.broadcast_to(value, (lax.axis_size(axis), *value.shape))
    return lax.all_to_all(copies, axis, split_axis=0, concat_axis=0, tiled=True)


def folded_in_pairs(pieces, combine):
    while len(jax.tree.leaves(pieces)[0]) > 1:
        pieces = jax.vmap(combine)(*(pieces[side::2] for side in (0, 1)))
    return pieces[0]


def entering(value, axis, combine, identity):
    count, mine = (lax.axis_size(axis), lax.axis_index(axis))
    passed = jnp.arange(count) < mine

    def kept(part, zero, own):
        part = jnp.where(
            passed.reshape(-1, *(1 for _ in own.shape)), part, jnp.asarray(zero, own.dtype)
        )
        return part

    pieces = copy_for_each(value, axis)
    return folded_in_pairs(kept(pieces, identity, value), combine)


def side_by_side(arrays, axis, split_dim, concat_dim, along):
    ends, at = ([], 0)
    for a in arrays[:-1]:
        at += a.shape[along]
        ends.append(at)
    both = jnp.concatenate(arrays, axis=along)
    return tuple(
        jnp.split(
            lax.all_to_all(both, axis, split_axis=split_dim, concat_axis=concat_dim, tiled=True),
            ends,
            axis=along,
        )
    )


def side_by_side_2(arrays, axis, dim, along):
    widths = [a.shape[along] for a in arrays]
    both = jnp.concatenate(arrays, axis=along)
    out = lax.all_gather(both, axis, axis=dim, tiled=True)
    return tuple(jnp.split(out, [sum(widths[:k]) for k in range(1, len(widths))], axis=along))


def expert_pass(packed_x, packed_g, gate_mat, up_mat, down_mat):
    pre_gate = jnp.dot(packed_x, gate_mat, preferred_element_type=jnp.float32)
    pre_up = jnp.dot(packed_x, up_mat, preferred_element_type=jnp.float32)
    sigmoid_part = jax.nn.sigmoid(SWISH_SLOPE * pre_gate)
    value = pre_gate * sigmoid_part
    slope_term = sigmoid_part + SWISH_SLOPE * pre_gate * sigmoid_part * (1.0 - sigmoid_part)
    hidden = (value * (pre_up + 1.0)).astype(jnp.bfloat16)
    out_term = lax.dot_general(
        hidden, down_mat, (((1,), (1,)), ((), ())), preferred_element_type=jnp.float32
    )
    d_hidden = jnp.dot(packed_g, down_mat, preferred_element_type=jnp.float32)
    d_gate = (d_hidden * (pre_up + 1.0) * slope_term).astype(jnp.bfloat16)
    d_up = (d_hidden * value).astype(jnp.bfloat16)
    return (out_term, hidden, d_gate, d_up)


def add_counts(earlier, later):
    return earlier + later


def body(tokens, cotangent, expert_ids, gate_weights, w_gate, w_up, w_down):
    sources = lax.axis_size("expert")
    local_experts = w_gate.shape[0]
    local_tokens, top_choices = expert_ids.shape
    model_width = tokens.shape[1]
    experts = sources * local_experts
    slot_count = 3 * local_tokens * top_choices // (2 * experts)
    assigns = local_tokens * top_choices
    flat_ids = expert_ids.reshape(assigns)
    expert_table = jnp.arange(experts, dtype=jnp.int32)
    onehot = (flat_ids[:, None] == expert_table[None, :]).astype(jnp.int32)
    local_rank = jnp.sum((jnp.cumsum(onehot, axis=0) - onehot) * onehot, axis=1)
    counts = jnp.sum(onehot, axis=0)
    offsets = entering(counts, "expert", add_counts, jnp.zeros_like(counts))
    bounds = jnp.stack([offsets, counts], axis=1).reshape(sources, local_experts, 2)
    bounds = lax.all_to_all(bounds, "expert", split_axis=0, concat_axis=0, tiled=True)
    start_rows = bounds[:, :, 0]
    live_rows = bounds[:, :, 1]
    slot_index = flat_ids * slot_count + local_rank
    token_index = jnp.arange(assigns, dtype=jnp.int32) // top_choices
    total_slots = experts * slot_count
    slot_token = jnp.zeros((total_slots,), jnp.int32).at[slot_index].set(token_index)
    slot_gate = (
        jnp.zeros((total_slots,), jnp.float32).at[slot_index].set(gate_weights.reshape(assigns))
    )
    slot_used = jnp.zeros((total_slots,), jnp.bool_).at[slot_index].set(True)
    send_tokens = jnp.where(slot_used[:, None], tokens[slot_token], jnp.zeros((), jnp.bfloat16))
    send_tokens = send_tokens.reshape(sources, local_experts * slot_count, model_width)
    send_cot = (slot_gate[:, None] * cotangent[slot_token].astype(jnp.float32)).astype(jnp.bfloat16)
    send_cot = send_cot.reshape(sources, local_experts * slot_count, model_width)
    recv_tokens, recv_cot = side_by_side((send_tokens, send_cot), "expert", 0, 0, 1)
    recv_tokens = recv_tokens.reshape(sources, local_experts, slot_count, model_width)
    recv_cot = recv_cot.reshape(sources, local_experts, slot_count, model_width)
    within = jnp.arange(slot_count, dtype=jnp.int32)
    position = start_rows[:, :, None] + within[None, None, :]
    kept_slot = (within[None, None, :] < live_rows[:, :, None]) & (position < CAP)
    target = jnp.where(kept_slot, position, CAP).astype(jnp.int32)
    owner_index = jnp.broadcast_to(
        jnp.arange(local_experts, dtype=jnp.int32)[None, :, None], target.shape
    )
    packed_x = (
        jnp.zeros((local_experts, CAP, model_width), jnp.bfloat16)
        .at[owner_index, target]
        .set(recv_tokens, mode="drop")
    )
    packed_g = (
        jnp.zeros((local_experts, CAP, model_width), jnp.bfloat16)
        .at[owner_index, target]
        .set(recv_cot, mode="drop")
    )
    full_gate, full_up = side_by_side_2((w_gate, w_up), "dp", 1, 0)
    full_down = lax.all_gather(w_down, "dp", axis=1, tiled=True)
    out_term, hidden, d_gate, d_up = expert_pass(
        packed_x[0], packed_g[0], full_gate[0], full_up[0], full_down[0]
    )
    out_terms = [out_term]
    hidden_list = [hidden]
    dgate_list = [d_gate]
    dup_list = [d_up]
    out_sum = jnp.stack(out_terms)
    hidden_all = jnp.stack(hidden_list)
    dgate_all = jnp.stack(dgate_list)
    dup_all = jnp.stack(dup_list)
    expert_out = out_sum.astype(jnp.bfloat16)
    fetched = expert_out[owner_index, jnp.minimum(target, CAP - 1)]
    send_back = jnp.where(kept_slot[..., None], fetched, jnp.zeros((), jnp.bfloat16))
    send_back = send_back.reshape(sources, local_experts * slot_count, model_width)
    returned = lax.all_to_all(send_back, "expert", split_axis=0, concat_axis=0, tiled=True).reshape(
        total_slots, model_width
    )
    per_assign = returned[slot_index]
    weighted = gate_weights.reshape(assigns)[:, None] * per_assign.astype(jnp.float32)
    mixed = jnp.sum(weighted.reshape(local_tokens, top_choices, model_width), axis=1).astype(
        jnp.bfloat16
    )
    grad_gate = jnp.einsum("lcd,lch->ldh", packed_x, dgate_all, preferred_element_type=jnp.float32)
    grad_up = jnp.einsum("lcd,lch->ldh", packed_x, dup_all, preferred_element_type=jnp.float32)
    grad_down = jnp.einsum("lcd,lch->ldh", packed_g, hidden_all, preferred_element_type=jnp.float32)
    summed = (
        lax.psum_scatter(
            grad_gate.astype(jnp.bfloat16), "dp", scatter_dimension=1, tiled=True
        ).astype(jnp.float32),
        lax.psum_scatter(
            grad_up.astype(jnp.bfloat16), "dp", scatter_dimension=1, tiled=True
        ).astype(jnp.float32),
        lax.psum_scatter(
            grad_down.astype(jnp.bfloat16), "dp", scatter_dimension=1, tiled=True
        ).astype(jnp.float32),
    )
    return (
        mixed,
        summed[0].astype(jnp.bfloat16),
        summed[1].astype(jnp.bfloat16),
        summed[2].astype(jnp.bfloat16),
    )


def solution(mesh):
    placed = (
        P(("expert", "dp"), None),
        P(("expert", "dp"), None),
        P(("expert", "dp"), None),
        P(("expert", "dp"), None),
        P("expert", "dp", None),
        P("expert", "dp", None),
        P("expert", "dp", None),
    )
    return jax.shard_map(
        body,
        mesh=mesh,
        in_specs=placed,
        out_specs=(
            P(("expert", "dp"), None),
            P("expert", "dp", None),
            P("expert", "dp", None),
            P("expert", "dp", None),
        ),
        check_vma=False,
    )
```

profile of v0, /device:TPU:55, one launch (start us, length us, event | category | flops | bytes accessed | tf_op | source)
XLA Modules:
  0.0 539.9 jit_solution(4664648111473070082)
XLA Ops:
  18.2 7.8 %all-to-all-start = ((s32[32,1,32]{2,1,0:T(1,128)}), s32[32,1,32]{2,1,0:T(1,128)S(1)}, u32[]{:S(2)}, u32[]{:S(2)}) async-start(s32[32,1,32]{2,1,0:T(1,128)} %broadcast_in_dim.69), calls=%async_computation | async-start | bytes 32768 | tf_op jit(solution)/shard_map/all_to_all | solution.py:14
  46.3 7.7 %all-to-all-start.1 = ((s32[32,1,2]{2,1,0:T(1,128)}), s32[32,1,2]{2,1,0:T(1,128)S(1)}, u32[]{:S(2)}, u32[]{:S(2)}) async-start(s32[32,1,2]{2,1,0:T(1,128)} %copy.50), calls=%async_computation.1 | async-start | bytes 32768 | tf_op jit(solution)/shard_map/all_to_all | solution.py:94
  54.1 4.5 pad_maximum_fusion
  58.6 8.1 %all-to-all-start.2 = ((bf16[32,48,1440]{2,1,0:T(8,128)(2,1)}), bf16[32,48,1440]{2,1,0:T(8,128)(2,1)}, u32[]{:S(2)}, u32[]{:S(2)}) async-start(bf16[32,48,1440]{2,1,0:T(8,128)(2,1)} %pad_maximum_fusion), calls=%async_computation.2 | async-start | bytes 9437184 | tf_op jit(solution)/shard_map/all_to_all | solution.py:45
  69.6 122.8 %all-to-all-done.2 = bf16[32,48,1440]{2,1,0:T(8,128)(2,1)} async-done(((bf16[32,48,1440]{2,1,0:T(8,128)(2,1)}), bf16[32,48,1440]{2,1,0:T(8,128)(2,1)}, u32[]{:S(2)}, u32[]{:S(2)}) %all-to-all-start.2) | async-done | bytes 4423712 | tf_op jit(solution)/shard_map/all_to_all | solution.py:45
  192.5 4.1 fusion.55
  196.5 20.2 %scatter_custom_fusion.3 = bf16[512,1440]{1,0:T(8,128)(2,1)} fusion(s32[768]{0:T(1024)S(1)} %reshape.444, bf16[768,1440]{1,0:T(8,128)(2,1)} %bitcast.100, bf16[]{:T(256)} %constant.22.clone.1), kind=kCustom, calls=%fused_computation.44 | custom fusion | bytes 1475072 | tf_op jit(solution)/shard_map/scatter | solution.py:122
  216.7 7.1 %scatter_custom_fusion.4 = bf16[512,1440]{1,0:T(8,128)(2,1)} fusion(s32[768]{0:T(1024)S(1)} %reshape.444, bf16[768,1440]{1,0:T(8,128)(2,1)S(1)} %bitcast.99, bf16[]{:T(256)} %constant.22.clone.1), kind=kCustom, calls=%fused_computation.42 | custom fusion | bytes 1474562 | tf_op jit(solution)/shard_map/scatter | solution.py:127
  223.8 8.1 %fusion.9 = f32[512,1440]{0,1:T(8,128)} fusion(bf16[512,1440]{1,0:T(8,128)(2,1)} %scatter_custom_fusion.4, bf16[1,1440,1440]{2,0,1:T(2,128)(2,1)} %all-gather.5.cloned.1.call-done), kind=kOutput, calls=%fused_computation.22 | convolution fusion | flops 2123366400 | bytes 8570880 | tf_op jit(solution)/shard_map/dot_general | solution.py:69
  231.9 18.4 %fusion.54 = (bf16[1,1440,1440]{2,0,1:T(2,128)(2,1)}, bf16[1,1440,1440]{2,0,1:T(2,128)(2,1)S(1)}) fusion(bf16[2,1440,1440]{2,0,1:T(2,128)(2,1)} %all-gather.3.cloned.1.call-done), kind=kLoop, calls=%fused_computation.106 | loop fusion | bytes 16588800 | tf_op jit(solution)/shard_map/split | solution.py:56
  250.4 6.0 %fusion.8 = f32[512,1440]{0,1:T(8,128)S(1)} fusion(bf16[512,1440]{1,0:T(8,128)(2,1)S(1)} %copy-done, bf16[1,1440,1440]{2,0,1:T(2,128)(2,1)} %get-tuple-element.22), kind=kOutput, calls=%fused_computation.21 | convolution fusion | flops 2123366400 | bytes 8570880 | tf_op jit(solution)/shard_map/dot_general | solution.py:60
  256.4 4.8 multiply_convert_fusion.2
  261.2 4.9 fusion.5
  269.3 11.9 %gather_fusion.2 = bf16[768,1440]{1,0:T(8,128)(2,1)} fusion(bf16[1,512,1440]{2,1,0:T(8,128)(2,1)S(1)} %copy.62, s32[768]{0:T(1024)S(1)} %reshape.400), kind=kCustom, calls=%fused_computation.2 | custom fusion | bytes 4429824 | tf_op jit(solution)/shard_map/gather | solution.py:143
  284.4 18.9 %all-to-all-start.3 = ((bf16[32,24,1440]{2,1,0:T(8,128)(2,1)}), bf16[32,24,1440]{2,1,0:T(8,128)(2,1)S(1)}, u32[]{:S(2)}, u32[]{:S(2)}) async-start(bf16[32,24,1440]{2,1,0:T(8,128)(2,1)} %broadcast_select_fusion.1), calls=%async_computation.3 | async-start | bytes 4718592 | tf_op jit(solution)/shard_map/all_to_all | solution.py:146
  303.4 8.0 %fusion.4 = bf16[1,1440,1440]{2,1,0:T(8,128)(2,1)} fusion(bf16[512,1440]{1,0:T(8,128)(2,1)} %scatter_custom_fusion.3, f32[512,1440]{0,1:T(8,128)} %fusion.9, f32[512,1440]{0,1:T(8,128)} %copy-done.12), kind=kOutput, calls=%fused_computation.13 | convolution fusion | flops 2130600960 | bytes 11520000 | tf_op jit(solution)/shard_map/lcd,lch->ldh/dot_general | solution.py:155
  311.5 5.0 fusion.3
  316.5 162.5 %fusion.53 = (bf16[184,1440]{1,0:T(8,128)(2,1)}, bf16[184,1440]{1,0:T(8,128)(2,1)S(1)}, bf16[184,1440]{1,0:T(8,128)(2,1)S(1)}) fusion(bf16[1,1440,1440]{2,1,0:T(8,128)(2,1)} %fusion.3, bf16[1,1440,1440]{2,1,0:T(8,128)(2,1)} %fusion.4, bf16[1,1440,1440]{2,1,0:T(8,128)(2,1)} %fusion.5), kind=kCustom, calls=%all-reduce-scatter.3 | all-reduce-scatter fusion | flops 6359041 | bytes 14032384
  479.9 5.3 collective-permute-start
  485.9 7.4 %collective-permute-start.1 = (bf16[28,1440]{1,0:T(8,128)(2,1)}, bf16[28,1440]{1,0:T(8,128)(2,1)}, u32[]{:S(2)}, u32[]{:S(2)}) collective-permute-start(bf16[28,1440]{1,0:T(8,128)(2,1)} %slice.78), channel_id=1, source_target_pairs={{0,1},{1,2},{2,3},{3,4},{4,5},{5,6},{6,7},{8,9},{9,10},{10,11},{11... | collective-permute-start | bytes 241928
  493.9 6.5 %collective-permute-start.2 = (bf16[28,1440]{1,0:T(8,128)(2,1)}, bf16[28,1440]{1,0:T(8,128)(2,1)}, u32[]{:S(2)}, u32[]{:S(2)}) collective-permute-start(bf16[28,1440]{1,0:T(8,128)(2,1)} %slice.79), channel_id=1, source_target_pairs={{0,1},{1,2},{2,3},{3,4},{4,5},{5,6},{6,7},{8,9},{9,10},{10,11},{11... | collective-permute-start | bytes 241928
  500.4 6.0 %concatenate.21 = bf16[212,1440]{1,0:T(8,128)(2,1)} concatenate(bf16[28,1440]{1,0:T(8,128)(2,1)} %collective-permute-done, bf16[184,1440]{1,0:T(8,128)(2,1)} %get-tuple-element.19), dimensions={0} | concatenate | bytes 1221120
  506.5 5.1 concatenate.22
  511.5 5.1 concatenate.23
  (124 shorter events, 58.0 us)
Async XLA Ops:
  7.2 216.7 %all-gather.5.cloned.1.call-start = ((), (), s32[]{:S(2)}) async-start(), calls=%async_computation.5 | async-start | bytes 9953280 | tf_op jit(solution)/shard_map/all_gather | solution.py:130
  10.2 221.7 %all-gather.3.cloned.1.call-start = ((), (), s32[]{:S(2)}) async-start(), calls=%async_computation.4 | async-start | bytes 9953280 | tf_op jit(solution)/shard_map/all_gather | solution.py:55
  11.2 14.8 %copy-start.6 = (bf16[128,1440]{0,1:T(8,128)(2,1)S(1)}, bf16[128,1440]{0,1:T(8,128)(2,1)}, u32[]{:S(2)}) copy-start(bf16[128,1440]{0,1:T(8,128)(2,1)} %param.8) | copy-start | bytes 1105924
  12.1 14.4 %copy-start.9 = (f32[128,4]{0,1:T(4,128)S(1)}, f32[128,4]{0,1:T(4,128)}, u32[]{:S(2)}) copy-start(f32[128,4]{0,1:T(4,128)} %param.10) | copy-start | bytes 6148
  12.1 19.9 %copy-start.7 = (bf16[128,1440]{0,1:T(8,128)(2,1)S(1)}, bf16[128,1440]{0,1:T(8,128)(2,1)}, u32[]{:S(2)}) copy-start(bf16[128,1440]{0,1:T(8,128)(2,1)} %param.7) | copy-start | bytes 1105924
  18.2 27.1 %all-to-all-start = ((s32[32,1,32]{2,1,0:T(1,128)}), s32[32,1,32]{2,1,0:T(1,128)S(1)}, u32[]{:S(2)}, u32[]{:S(2)}) async-start(s32[32,1,32]{2,1,0:T(1,128)} %broadcast_in_dim.69), calls=%async_computation | async-start | bytes 32768 | tf_op jit(solution)/shard_map/all_to_all | solution.py:14
  26.5 5.3 copy-start.3
  46.3 12.3 %all-to-all-start.1 = ((s32[32,1,2]{2,1,0:T(1,128)}), s32[32,1,2]{2,1,0:T(1,128)S(1)}, u32[]{:S(2)}, u32[]{:S(2)}) async-start(s32[32,1,2]{2,1,0:T(1,128)} %copy.50), calls=%async_computation.1 | async-start | bytes 32768 | tf_op jit(solution)/shard_map/all_to_all | solution.py:94
  58.6 8.1 %copy-start.10 = (u32[256]{0:T(256)S(1)}, u32[256]{0:T(256)}, u32[]{:S(2)}) copy-start(u32[256]{0:T(256)} %constant.89) | copy-start | bytes 3076
  58.6 133.9 %all-to-all-start.2 = ((bf16[32,48,1440]{2,1,0:T(8,128)(2,1)}), bf16[32,48,1440]{2,1,0:T(8,128)(2,1)}, u32[]{:S(2)}, u32[]{:S(2)}) async-start(bf16[32,48,1440]{2,1,0:T(8,128)(2,1)} %pad_maximum_fusion), calls=%async_computation.2 | async-start | bytes 9437184 | tf_op jit(solution)/shard_map/all_to_all | solution.py:45
  231.9 18.4 %copy-start = (bf16[512,1440]{1,0:T(8,128)(2,1)S(1)}, bf16[512,1440]{1,0:T(8,128)(2,1)}, u32[]{:S(2)}) copy-start(bf16[512,1440]{1,0:T(8,128)(2,1)} %scatter_custom_fusion.3) | copy-start | bytes 4423684
  256.4 4.8 copy-start.12
  256.4 4.8 copy-start.2
  256.4 9.7 %slice-start = ((s8[8847360]{0:T(1024)(128)(4,1)}), s8[458752]{0:T(1024)(128)(4,1)S(1)}, s32[]{:S(2)}) async-start(s8[8847360]{0:T(1024)(128)(4,1)} %bitcast.108), calls=%async_computation.6 | async-start | bytes 917504
  256.4 9.7 %slice-start.1 = ((s8[8847360]{0:T(1024)(128)(4,1)}), s8[4194304]{0:T(1024)(128)(4,1)S(1)}, s32[]{:S(2)}) async-start(s8[8847360]{0:T(1024)(128)(4,1)} %bitcast.108), calls=%async_computation.7 | async-start | bytes 8388608
  261.2 4.9 slice-start.2
  284.4 238.2 %all-to-all-start.3 = ((bf16[32,24,1440]{2,1,0:T(8,128)(2,1)}), bf16[32,24,1440]{2,1,0:T(8,128)(2,1)S(1)}, u32[]{:S(2)}, u32[]{:S(2)}) async-start(bf16[32,24,1440]{2,1,0:T(8,128)(2,1)} %broadcast_select_fusion.1), calls=%async_computation.3 | async-start | bytes 4718592 | tf_op jit(solution)/shard_map/all_to_all | solution.py:146
  303.4 8.1 %copy-start.1 = (bf16[512,1440]{1,0:T(8,128)(2,1)S(1)}, bf16[512,1440]{1,0:T(8,128)(2,1)}, u32[]{:S(2)}) copy-start(bf16[512,1440]{1,0:T(8,128)(2,1)} %scatter_custom_fusion.3) | copy-start | bytes 4423684
  303.4 8.1 %copy-start.11 = (f32[512,1440]{0,1:T(8,128)S(1)}, f32[512,1440]{0,1:T(8,128)}, u32[]{:S(2)}) copy-start(f32[512,1440]{0,1:T(8,128)} %fusion.9) | copy-start | bytes 8847364
  303.4 8.1 %copy-start.13 = (f32[512,1440]{0,1:T(8,128)S(1)}, f32[512,1440]{0,1:T(8,128)}, u32[]{:S(2)}) copy-start(f32[512,1440]{0,1:T(8,128)} %copy-done.12) | copy-start | bytes 8847364
  303.4 8.1 %copy-start.14 = (f32[512,1440]{0,1:T(8,128)S(1)}, f32[512,1440]{0,1:T(8,128)}, u32[]{:S(2)}) copy-start(f32[512,1440]{0,1:T(8,128)} %get-tuple-element.29) | copy-start | bytes 8847364
  479.9 20.6 %collective-permute-start = (bf16[28,1440]{1,0:T(8,128)(2,1)S(1)}, bf16[28,1440]{1,0:T(8,128)(2,1)}, u32[]{:S(2)}, u32[]{:S(2)}) collective-permute-start(bf16[28,1440]{1,0:T(8,128)(2,1)S(1)} %slice.77), channel_id=1, source_target_pairs={{0,1},{1,2},{2,3},{3,4},{4,5},{5,6},{6,7},{8,9},{9,10},{10,11},{11... | collective-permute-start | bytes 241928
  485.9 20.6 %collective-permute-start.1 = (bf16[28,1440]{1,0:T(8,128)(2,1)}, bf16[28,1440]{1,0:T(8,128)(2,1)}, u32[]{:S(2)}, u32[]{:S(2)}) collective-permute-start(bf16[28,1440]{1,0:T(8,128)(2,1)} %slice.78), channel_id=1, source_target_pairs={{0,1},{1,2},{2,3},{3,4},{4,5},{5,6},{6,7},{8,9},{9,10},{10,11},{11... | collective-permute-start | bytes 241928
  493.9 17.6 %collective-permute-start.2 = (bf16[28,1440]{1,0:T(8,128)(2,1)}, bf16[28,1440]{1,0:T(8,128)(2,1)}, u32[]{:S(2)}, u32[]{:S(2)}) collective-permute-start(bf16[28,1440]{1,0:T(8,128)(2,1)} %slice.79), channel_id=1, source_target_pairs={{0,1},{1,2},{2,3},{3,4},{4,5},{5,6},{6,7},{8,9},{9,10},{10,11},{11... | collective-permute-start | bytes 241928
  (3 other events, 11.6 us)
Sparse Core Ops, SparseCore 0:
  10.4 105.9 all-gather.4
  118.1 98.5 all-gather.2
where the time goes:
time: 548 us; the launch traced here: 540 us
  blocking collectives  162 us (30%)
  waiting for transfers between devices  123 us (22%)
  local copies, waits for them, and re-layouts  118 us (22%)
  starting transfers between devices  61.8 us (11%)
  matrix products  39.2 us (7%)
  other arithmetic  20 us (4%)
  between operations  15.7 us (3%)
    unnamed x1, blocking collectives  162 us
    all_to_all x1, waiting for transfers between devices, side_by_side(): lax.all_to_all(both, axis, split_axis=split_dim, concat_axis=concat_dim,...  123 us
    unnamed x54, local copies, waits for them, and re-layouts  31.3 us
    scatter x1, local copies, waits for them, and re-layouts, body(): packed_x = jnp.zeros((local_experts, CAP, model_width), jnp.bfloat16).at[...  20.2 us
    unnamed x3, starting transfers between devices  19.2 us
    all_to_all x1, starting transfers between devices, body(): lax.all_to_all(send_back, 'expert', split_axis=0, concat_axis=0, tiled=True)  18.9 us
    split x1, local copies, waits for them, and re-layouts, side_by_side_2(): jnp.split(out, [sum(widths[:k]) for k in range(1, len(widths))], axis=along)  18.4 us
    gather x1, local copies, waits for them, and re-layouts, body(): fetched = expert_out[owner_index, jnp.minimum(target, CAP - 1)]  11.9 us
  transfers between devices with their start and end apart: 9, of which 1 were waited for; matrix products, arithmetic and copies ran while one was open for 51% of the time, Pallas kernels for 0%

commit v1 on v0

v1 whole, which is shorter than its diff:
```python
import functools

import jax
import jax.numpy as jnp
from jax import lax
from jax.experimental import pallas as pl
from jax.experimental.pallas import tpu as pltpu
from jax.sharding import PartitionSpec as P

MESH = pl.DeviceIdType.MESH
SWISH_SLOPE = 1.702
F32, BF16 = jnp.float32, jnp.bfloat16
TOK = 128
CAP = 512
SLOT = 24
D = 1440
FH = 1440
OWN = 180
SENT = 184
CHUNK = 192
DP = 8 * CHUNK
PAIR = 2 * CHUNK
HALF = 96
SLOTS = 32 * SLOT
PLANE = 16 * SLOT
VM = functools.partial(pl.BlockSpec, memory_space=pltpu.VMEM)


def mul(value, k):
    return pl.multiple_of(value, k)


class Place:
    def __init__(self):
        e, d = lax.axis_index("expert"), lax.axis_index("dp")
        self.x, self.zl, self.y = e // 8, (e // 4) % 2, e % 4
        self.h, self.c = d // 2, d % 2
        self.e, self.d = e, d
        self.sibling = (e, self.h * 2 + 1 - self.c)
        self.up = (e, ((self.h + 1) % 4) * 2 + self.c)
        self.down = (e, ((self.h + 3) % 4) * 2 + self.c)
        self.partner = (self.x * 8 + (1 - self.zl) * 4 + self.y, d)
        self.p = self.x * 4 + self.y

    def plane(self, i, sign):
        px = (self.x + sign * (i // 4) + 4) % 4
        py = (self.y + sign * (i % 4) + 4) % 4
        return px * 4 + py, px, py

    def plane_device(self, px, py):
        return (px * 8 + self.zl * 4 + py, self.d)

    def block(self, px, py, bi):
        zb = self.zl if bi == 0 else 1 - self.zl
        return px * 8 + zb * 4 + py

    def greet(self):
        barrier = pltpu.get_barrier_semaphore()
        for peer in (self.sibling, self.up, self.down, self.partner):
            pl.semaphore_signal(barrier, inc=1, device_id=peer, device_id_type=MESH)

        @pl.loop(1, 16)
        def _(i):
            _, px, py = self.plane(i, 1)
            pl.semaphore_signal(
                barrier, inc=1, device_id=self.plane_device(px, py), device_id_type=MESH
            )

        pl.semaphore_wait(barrier, 19)


def remote(src, dst, ssem, rsem, device):
    return pltpu.make_async_remote_copy(
        src_ref=src, dst_ref=dst, send_sem=ssem, recv_sem=rsem, device_id=device, device_id_type=MESH
    )


def rows_of(block, size=SLOT):
    return pl.ds(mul(block * SLOT, 8), size)


def dot(a, b):
    return jnp.dot(a, b, preferred_element_type=F32)


def dot_nt(a, b):
    return lax.dot_general(a, b, (((1,), (1,)), ((), ())), preferred_element_type=F32)


def dot_tn(a, b):
    return lax.dot_general(a, b, (((0,), (0,)), ((), ())), preferred_element_type=F32)


def one_zero(flag):
    return jnp.where(flag, 1.0, 0.0)


def gather_kernel(
    meta, tok, cot, wg_in, wu_in, wd_in,
    x_out, g_out, hid_out, dg_out, du_out, eo_out, r_out, mt_out,
    wg, wu, wd, zmeta, ztok, zcot, send_x, send_g, recv_x, recv_g, acc_g, acc_u, acc_d,
    loc_sem, zs, zr, ags, agr, ds_, dr,
):
    me = Place()
    h, c = me.h, me.c
    weights = (wg, wu, wd)

    def base(j, core):
        return CHUNK * (2 * j + core)

    def shard(w, j, core, lo=0, size=SENT):
        return w.at[pl.ds(mul(base(j, core) + lo, 8), size), :]

    own_copies = [
        pltpu.make_async_copy(
            src, w.at[pl.ds(mul(base(h, c), 8), SENT), :], loc_sem.at[a]
        )
        for a, (src, w) in enumerate(
            ((wg_in.at[pl.ds(0, SENT), :], wg), (wu_in.at[pl.ds(0, SENT), :], wu), (wd_in.at[pl.ds(0, SENT), :], wd))
        )
    ]
    for cp in own_copies:
        cp.start()
    for w in weights:
        for k in range(8):
            w[pl.ds(CHUNK * k + SENT, CHUNK - SENT), :] = jnp.zeros((CHUNK - SENT, FH), BF16)

    me.greet()

    zex = [
        remote(src, dst, zs.at[k], zr.at[k], me.partner)
        for k, (src, dst) in enumerate(((meta, zmeta), (tok, ztok), (cot, zcot)))
    ]
    for cp in zex:
        cp.start()

    def up_j(k):
        return (h + k) % 4

    def ag(a, k):
        w = weights[a]
        s, r = ags.at[a * 9 + k], agr.at[a * 9 + k]
        if k == 0:
            return remote(shard(w, h, c), shard(w, h, c), s, r, me.up)
        if k == 1:
            return remote(shard(w, h, c), shard(w, h, c), s, r, me.down)
        if k == 2:
            return remote(shard(w, h, c), shard(w, h, c), s, r, me.sibling)
        if k == 3:
            part = shard(w, up_j(3), c, 0, HALF)
            return remote(part, part, s, r, me.up)
        if k == 4:
            part = shard(w, up_j(1), c, HALF, SENT - HALF)
            return remote(part, part, s, r, me.down)
        if k in (5, 6):
            part = shard(w, up_j(3 if k == 5 else 1), c)
            return remote(part, part, s, r, me.sibling)
        part = shard(w, up_j(2), c, 0, HALF) if k == 7 else shard(w, up_j(2), c, HALF, SENT - HALF)
        return remote(part, part, s, r, me.sibling)

    def ag_in(a, k):
        w = weights[a]
        s, r = ags.at[a * 9 + k], agr.at[a * 9 + k]
        lo, size = 0, SENT
        if k == 0:
            j, core = up_j(3), c
        elif k == 1:
            j, core = up_j(1), c
        elif k == 2:
            j, core = h, 1 - c
        elif k == 3:
            j, core, size = up_j(2), c, HALF
        elif k == 4:
            j, core, lo, size = up_j(2), c, HALF, SENT - HALF
        elif k in (5, 6):
            j, core = up_j(3 if k == 5 else 1), 1 - c
        elif k == 7:
            j, core, size = up_j(2), 1 - c, HALF
        else:
            j, core, lo, size = up_j(2), 1 - c, HALF, SENT - HALF
        part = shard(w, j, core, lo, size)
        return remote(part, part, s, r, me.sibling)

    for a in (0, 1):
        own_copies[a].wait()
        for k in (0, 1, 2):
            ag(a, k).start()
    own_copies[2].wait()

    def dispatch_copy(bi, i, incoming):
        sign = -1 if incoming else 1
        p, px, py = me.plane(i, sign)
        at = (bi * 16 + p) * SLOT
        source = me.block(px, py, bi) if incoming else me.block(me.x, me.y, bi)
        copies = []
        for arr, (src, dst) in enumerate(((send_x, recv_x), (send_g, recv_g))):
            k = (bi * 2 + arr) * 16 + i
            copies.append(
                remote(
                    src.at[pl.ds(mul(at, 8), SLOT), :],
                    dst.at[rows_of(source), :],
                    ds_.at[k],
                    dr.at[k],
                    me.plane_device(px, py),
                )
            )
        return copies

    def dispatch(bi, m_ref, t_ref, c_ref):
        place = lax.broadcasted_iota(jnp.int32, (16, TOK), 0)
        expert = ((place // 4) * 8 + me.zl * 4 + place % 4).astype(F32)
        named = jnp.zeros((16, TOK), F32)
        gates = jnp.zeros((16, TOK), F32)
        for k in range(4):
            hit = m_ref[k : k + 1, :] == expert
            named = named + one_zero(hit)
            gates = gates + jnp.where(hit, m_ref[4 + k : 5 + k, :], 0.0)
        earlier = one_zero(
            lax.broadcasted_iota(jnp.int32, (TOK, TOK), 0) < lax.broadcasted_iota(jnp.int32, (TOK, TOK), 1)
        ).astype(BF16)
        rank = dot(named.astype(BF16), earlier)
        rank = jnp.where(named > 0.5, rank, -1.0)
        slot = lax.broadcasted_iota(jnp.int32, (16, SLOT, TOK), 1).astype(F32)
        chosen3 = one_zero(slot == rank[:, None, :])
        chosen = chosen3.reshape(PLANE, TOK)
        weighted = (chosen3 * gates[:, None, :]).reshape(PLANE, TOK)
        mt_out[bi] = weighted
        slot_gate = jnp.sum(weighted, axis=1, keepdims=True)
        pick = chosen.astype(BF16)
        send_x[pl.ds(bi * PLANE, PLANE), :] = dot(pick, t_ref[...]).astype(BF16)
        send_g[pl.ds(bi * PLANE, PLANE), :] = (dot(pick, c_ref[...]) * slot_gate).astype(BF16)
        mine = rows_of(me.block(me.x, me.y, bi))
        here = pl.ds(mul((bi * 16 + me.p) * SLOT, 8), SLOT)
        recv_x[mine, :] = send_x[here, :]
        recv_g[mine, :] = send_g[here, :]

        @pl.loop(1, 16)
        def _(i):
            for cp in dispatch_copy(bi, i, False):
                cp.start()

    dispatch(0, meta, tok, cot)
    for cp in zex:
        cp.wait_recv()
    dispatch(1, zmeta, ztok, zcot)

    def forward_neighbours(a):
        ag_in(a, 0).wait_recv()
        ag(a, 3).start()
        ag(a, 5).start()
        ag_in(a, 1).wait_recv()
        ag(a, 4).start()
        ag(a, 6).start()

    forward_neighbours(0)
    forward_neighbours(1)
    for k in (0, 1, 2):
        ag(2, k).start()

    for bi in range(2):

        @pl.loop(1, 16)
        def _(i):
            for cp in dispatch_copy(bi, i, True):
                cp.wait_recv()

    eye_lane = one_zero(lax.broadcasted_iota(jnp.int32, (8, 128), 1) == OWN - 128).astype(BF16)
    flags = dot_nt(eye_lane, recv_x[:, 128:256])
    before = one_zero(
        lax.broadcasted_iota(jnp.int32, (SLOTS, SLOTS), 0) < lax.broadcasted_iota(jnp.int32, (SLOTS, SLOTS), 1)
    ).astype(BF16)
    position = dot(flags.astype(BF16), before)
    position = jnp.where(flags > 0.5, position, -1.0)[0:1, :]

    @pl.loop(0, 2)
    def _(m):
        at = mul(m * 256, 256)
        row = (lax.broadcasted_iota(jnp.int32, (256, SLOTS), 0) + at).astype(F32)
        pick = one_zero(row == position).astype(BF16)
        r_out[pl.ds(at, 256), :] = pick
        x_out[pl.ds(at, 256), :] = dot(pick, recv_x[...]).astype(BF16)
        g_out[pl.ds(at, 256), :] = dot(pick, recv_g[...]).astype(BF16)

    def project(j, first):
        cols = pl.ds(mul(j * PAIR, 128), PAIR)

        @pl.loop(0, 2)
        def _(m):
            rows = pl.ds(mul(m * 256, 256), 256)
            xs = x_out[rows, cols]
            for acc, w in ((acc_g, wg), (acc_u, wu)):
                part = dot(xs, w[cols, :])
                acc[rows, :] = part if first else acc[rows, :] + part

    for a in (0, 1):
        ag_in(a, 2).wait_recv()
    project(h, True)
    for a in (0, 1):
        ag_in(a, 5).wait_recv()
    project(up_j(3), False)
    for a in (0, 1):
        ag_in(a, 6).wait_recv()
    project(up_j(1), False)

    def finish_gather(a):
        ag_in(a, 3).wait_recv()
        ag(a, 7).start()
        ag_in(a, 4).wait_recv()
        ag(a, 8).start()

    def wait_opposite(a):
        ag_in(a, 7).wait_recv()
        ag_in(a, 8).wait_recv()

    finish_gather(0)
    finish_gather(1)
    wait_opposite(0)
    wait_opposite(1)
    project(up_j(2), False)

    @pl.loop(0, 16)
    def _(m):
        rows = pl.ds(mul(m * 32, 32), 32)
        gate, up = acc_g[rows, :], acc_u[rows, :] + 1.0
        sg = jax.nn.sigmoid(SWISH_SLOPE * gate)
        value = gate * sg
        slope = sg + SWISH_SLOPE * value * (1.0 - sg)
        hid_out[rows, :] = (value * up).astype(BF16)
        acc_g[rows, :] = up * slope
        acc_u[rows, :] = value

    def down_step(j, first):
        cols = pl.ds(mul(j * PAIR, 128), PAIR)

        @pl.loop(0, 2)
        def _(m):
            rows = pl.ds(mul(m * 256, 256), 256)
            part = dot(g_out[rows, cols], wd[cols, :])
            acc_d[rows, :] = part if first else acc_d[rows, :] + part

    def out_step(j):
        cols = pl.ds(mul(j * PAIR, 128), PAIR)

        @pl.loop(0, 2)
        def _(m):
            rows = pl.ds(mul(m * 256, 256), 256)
            eo_out[rows, cols] = dot_nt(hid_out[rows, :], wd[cols, :]).astype(BF16)

    forward_neighbours(2)
    ag_in(2, 2).wait_recv()
    down_step(h, True)
    out_step(h)
    ag_in(2, 5).wait_recv()
    down_step(up_j(3), False)
    out_step(up_j(3))
    ag_in(2, 6).wait_recv()
    down_step(up_j(1), False)
    out_step(up_j(1))
    finish_gather(2)
    wait_opposite(2)
    down_step(up_j(2), False)
    out_step(up_j(2))

    @pl.loop(0, 16)
    def _(m):
        rows = pl.ds(mul(m * 32, 32), 32)
        dh = acc_d[rows, :]
        dg_out[rows, :] = (dh * acc_g[rows, :]).astype(BF16)
        du_out[rows, :] = (dh * acc_u[rows, :]).astype(BF16)

    for cp in zex:
        cp.wait_send()
    for a in range(3):
        for k in range(9):
            ag(a, k).wait_send()
    for bi in range(2):

        @pl.loop(1, 16)
        def _(i):
            for cp in dispatch_copy(bi, i, False):
                cp.wait_send()


def reduce_kernel(
    x, g, hid, dg, du, eo, r_mat, mt,
    gg_out, gu_out, gd_out, mixed_out,
    pd, pg, pu, ra, hs, hr, fs, fr, rets, rr, zsend, zrecv,
    d2s, d2r, hss, hsr, fss, fsr, rs, rr_sem, zs, zr,
):
    me = Place()
    h, c = me.h, me.c
    arrays = ((pd, g, hid), (pg, x, dg), (pu, x, du))
    outs = (gd_out, gg_out, gu_out)

    def up_j(k):
        return (h + k) % 4

    def part_rows(j, core):
        return pl.ds(mul(CHUNK * (2 * j + core), 8), SENT)

    def exchange(a, k):
        return remote(
            arrays[a][0].at[part_rows(up_j(k), 1 - c), :],
            ra.at[a * 4 + k],
            d2s.at[a * 4 + k],
            d2r.at[a * 4 + k],
            me.sibling,
        )

    def half(a, k):
        lo, size = ((0, HALF), (HALF, SENT - HALF))[k]
        return remote(
            hs.at[a, pl.ds(lo, size), :],
            hr.at[a, pl.ds(lo, size), :],
            hss.at[a * 2 + k],
            hsr.at[a * 2 + k],
            (me.up, me.down)[k],
        )

    def full(a, k):
        return remote(
            fs.at[a * 2 + k], fr.at[a * 2 + k], fss.at[a * 2 + k], fsr.at[a * 2 + k], (me.up, me.down)[k]
        )

    def back_copy(bi, i, incoming):
        p, px, py = me.plane(i, -1 if incoming else 1)
        place = p if incoming else me.p
        k = bi * 16 + i
        return remote(
            rets.at[rows_of(me.block(px, py, bi)), :],
            rr.at[pl.ds(mul((bi * 16 + place) * SLOT, 8), SLOT), :],
            rs.at[k],
            rr_sem.at[k],
            me.plane_device(px, py),
        )

    me.greet()

    for a in range(3):
        parts, left, right = arrays[a]
        for k in (2, 1, 3, 0):
            cols = pl.ds(mul(up_j(k) * PAIR, 128), PAIR)
            parts[cols, :] = dot_tn(left[:, cols], right[...]).astype(BF16)
            exchange(a, k).start()
        exchange(a, 2).wait_recv()
        mine = parts[part_rows(up_j(2), c), :]
        hs[a] = (mine.astype(F32) + ra[a * 4 + 2].astype(F32)).astype(BF16)
        half(a, 0).start()
        half(a, 1).start()
        if a == 0:

            @pl.loop(0, 2)
            def _(m):
                cols = pl.ds(mul(m * PLANE, 128), PLANE)
                rets[pl.ds(mul(m * PLANE, 8), PLANE), :] = dot_tn(r_mat[:, cols], eo[...]).astype(BF16)

            for bi in range(2):
                rr[pl.ds(mul((bi * 16 + me.p) * SLOT, 8), SLOT), :] = rets[
                    rows_of(me.block(me.x, me.y, bi)), :
                ]

                @pl.loop(1, 16)
                def _(i):
                    back_copy(bi, i, False).start()

    for a in range(3):
        parts = arrays[a][0]
        for k, jj in ((0, 1), (1, 3)):
            exchange(a, jj).wait_recv()
            half(a, k).wait_recv()
            total = parts[part_rows(up_j(jj), c), :].astype(F32) + ra[a * 4 + jj].astype(F32)
            lo, size = ((0, HALF), (HALF, SENT - HALF))[k]
            fs[a * 2 + k] = total.astype(BF16)
            fs[a * 2 + k, pl.ds(lo, size), :] = (
                total[lo : lo + size] + hr[a, pl.ds(lo, size), :].astype(F32)
            ).astype(BF16)
            full(a, k).start()

    for bi in range(2):

        @pl.loop(1, 16)
        def _(i):
            back_copy(bi, i, True).wait_recv()

    def combine(bi):
        weight = mt[bi]
        high = weight.astype(BF16)
        low = (weight - high.astype(F32)).astype(BF16)
        got = rr[pl.ds(bi * PLANE, PLANE), :]
        return dot_tn(high, got) + dot_tn(low, got)

    zsend[...] = combine(1).astype(BF16)
    zcopy = remote(zsend, zrecv, zs.at[0], zr.at[0], me.partner)
    zcopy.start()
    own = combine(0)
    zcopy.wait_recv()
    mixed_out[...] = (own + zrecv[...].astype(F32)).astype(BF16)

    for a in range(3):
        parts = arrays[a][0]
        exchange(a, 0).wait_recv()
        total = parts[part_rows(h, c), :].astype(F32) + ra[a * 4].astype(F32)
        for k in range(2):
            full(a, k).wait_recv()
            total = total + fr[a * 2 + k].astype(F32)
        outs[a][...] = total.astype(BF16)

    zcopy.wait_send()
    for a in range(3):
        for k in range(4):
            exchange(a, k).wait_send()
        for k in range(2):
            half(a, k).wait_send()
            full(a, k).wait_send()
    for bi in range(2):

        @pl.loop(1, 16)
        def _(i):
            back_copy(bi, i, False).wait_send()


def sds(shape, dtype=BF16):
    return jax.ShapeDtypeStruct(shape, dtype)


def widened(a):
    return jnp.pad(a.reshape(TOK, 8, OWN), ((0, 0), (0, 0), (0, CHUNK - OWN))).reshape(TOK, DP)


def body(tokens, cotangent, expert_ids, gate_weights, w_gate, w_up, w_down):
    lane = lax.broadcasted_iota(jnp.int32, (TOK, DP), 1)
    tok = jnp.where(lane == OWN, jnp.ones((), BF16), widened(tokens))
    cot = widened(cotangent)
    meta = jnp.concatenate([expert_ids.astype(F32), gate_weights], axis=1).T
    shards = [jnp.pad(w[0], ((0, CHUNK - OWN), (0, 0))) for w in (w_gate, w_up, w_down)]
    dma, reg = pltpu.SemaphoreType.DMA, pltpu.SemaphoreType.REGULAR
    mids = pl.pallas_call(
        gather_kernel,
        name="gather",
        out_shape=[
            sds((CAP, DP)), sds((CAP, DP)), sds((CAP, FH)), sds((CAP, FH)), sds((CAP, FH)), sds((CAP, DP)),
            sds((CAP, SLOTS)), sds((2, PLANE, TOK), F32),
        ],
        in_specs=[VM(), VM(), VM()] + [pl.BlockSpec(memory_space=pl.ANY)] * 3,
        out_specs=[VM()] * 8,
        scratch_shapes=[
            pltpu.VMEM((DP, FH), BF16), pltpu.VMEM((DP, FH), BF16), pltpu.VMEM((DP, FH), BF16),
            pltpu.VMEM((8, TOK), F32), pltpu.VMEM((TOK, DP), BF16), pltpu.VMEM((TOK, DP), BF16),
            pltpu.VMEM((SLOTS, DP), BF16), pltpu.VMEM((SLOTS, DP), BF16),
            pltpu.VMEM((SLOTS, DP), BF16), pltpu.VMEM((SLOTS, DP), BF16),
            pltpu.VMEM((CAP, FH), F32), pltpu.VMEM((CAP, FH), F32), pltpu.VMEM((CAP, FH), F32),
            dma((3,)), dma((3,)), dma((3,)), dma((27,)), dma((27,)), dma((64,)), dma((64,)),
        ],
        compiler_params=pltpu.CompilerParams(
            collective_id=0, has_side_effects=True, vmem_limit_bytes=67043328
        ),
    )(meta, tok, cot, *shards)
    gg, gu, gd, mixed = pl.pallas_call(
        reduce_kernel,
        name="reduce",
        out_shape=[sds((SENT, FH)), sds((SENT, FH)), sds((SENT, FH)), sds((TOK, DP))],
        in_specs=[VM()] * 8,
        out_specs=[VM()] * 4,
        scratch_shapes=[
            pltpu.VMEM((DP, FH), BF16), pltpu.VMEM((DP, FH), BF16), pltpu.VMEM((DP, FH), BF16),
            pltpu.VMEM((12, SENT, FH), BF16),
            pltpu.VMEM((3, SENT, FH), BF16), pltpu.VMEM((3, SENT, FH), BF16),
            pltpu.VMEM((6, SENT, FH), BF16), pltpu.VMEM((6, SENT, FH), BF16),
            pltpu.VMEM((SLOTS, DP), BF16), pltpu.VMEM((SLOTS, DP), BF16),
            pltpu.VMEM((TOK, DP), BF16), pltpu.VMEM((TOK, DP), BF16),
            dma((12,)), dma((12,)), dma((6,)), dma((6,)), dma((6,)), dma((6,)),
            dma((32,)), dma((32,)), dma((1,)), dma((1,)),
        ],
        compiler_params=pltpu.CompilerParams(
            collective_id=1, has_side_effects=True, vmem_limit_bytes=67043328
        ),
    )(*mids)
    mixed = mixed.reshape(TOK, 8, CHUNK)[:, :, :OWN].reshape(TOK, D)
    return mixed, gg[None, :OWN], gu[None, :OWN], gd[None, :OWN]


def solution(mesh):
    rows, weight = P(("expert", "dp"), None), P("expert", "dp", None)
    return jax.shard_map(
        body,
        mesh=mesh,
        in_specs=(rows, rows, rows, rows, weight, weight, weight),
        out_specs=(rows, weight, weight, weight),
        check_vma=False,
    )
```

time: 548 us -> 299 us (0.55)
  the two profiles are of different devices: /device:TPU:55 before, /device:TPU:56 now
where the time goes in v1:
time: 299 us; the launch traced here: 298 us
  Pallas kernels  286 us (96%)
  local copies, waits for them, and re-layouts  8.99 us (3%)
    pallas_call x1, Pallas kernels, body(): pl.pallas_call(gather_kernel, name='gather', out_shape=[sds((CAP, DP)), s...  150 us
    pallas_call x1, Pallas kernels, body(): pl.pallas_call(reduce_kernel, name='reduce', out_shape=[sds((SENT, FH)),...  136 us

profile of v1, /device:TPU:56, one launch (start us, length us, event | category | flops | bytes accessed | tf_op | source)
XLA Modules:
  0.0 298.5 jit_solution(7055987920693874799)
XLA Ops:
  0.6 0.0 copy-start.6
  0.6 0.7 convert_element_type.10
  1.4 1.3 maximum_bitcast_fusion.meta
  2.7 1.1 reshape.26
  3.8 0.2 copy.14
  3.9 0.0 copy-start
  4.0 0.8 broadcast_select_fusion.tok
  4.7 0.0 copy-done.6
  4.7 0.1 reshape.28
  4.9 0.0 copy-start.2
  4.9 0.9 copy.15.cot
  5.8 0.0 copy-done
  5.8 0.9 pad.19.wg_in
  6.7 0.0 copy-done.1
  6.7 0.9 pad.20.wu_in
  7.5 0.0 copy-done.2
  7.5 0.9 pad.21.wd_in
  8.4 149.7 %gather.1 = (bf16[512,1536]{1,0:T(8,128)(2,1)}, bf16[512,1536]{1,0:T(8,128)(2,1)}, bf16[512,1440]{1,0:T(8,128)(2,1)}, bf16[512,1440]{1,0:T(8,128)(2,1)}, bf16[51...) custom-call(f32[8,128]{1,0:T(8,128)} %maximum_bitcast_fusion.meta, ...), custom_call_target="tpu_custom_call" | custom-call | tf_op jit(solution)/shard_map/gather/pallas_call | solution.py:537
  158.1 136.2 %reduce.1 = (bf16[184,1440]{1,0:T(8,128)(2,1)}, bf16[184,1440]{1,0:T(8,128)(2,1)}, bf16[184,1440]{1,0:T(8,128)(2,1)}, bf16[128,1536]{1,0:T(8,128)(2,1)}) custom-call(bf16[512,1536]{1,0:T(8,128)(2,1)} %get-tuple-element.16.x, bf16[512,1536]{1,0:T(8,128)(2,1)} %get-tuple-element.17.g, bf16[512,1440]{1,0:T(8,128)(2,1)} %get-tuple-element.18.hid, ...), custom_call_target="tpu_custom_call" | custom-call | tf_op jit(solution)/shard_map/reduce/pallas_call | solution.py:558
  294.4 1.3 copy.16
  295.7 0.8 reshape.31
  296.6 0.8 slice_bitcast_fusion.2
  297.4 0.0 copy-done.3
  297.4 1.1 slice_bitcast_fusion
  (10 shorter events, 0.1 us)
Async XLA Ops:
  0.6 4.1 %copy-start.6 = (bf16[128,1440]{0,1:T(8,128)(2,1)S(1)}, bf16[128,1440]{0,1:T(8,128)(2,1)}, u32[]{:S(2)}) copy-start(bf16[128,1440]{0,1:T(8,128)(2,1)} %param.8) | copy-start | bytes 1105924
  3.9 1.9 copy-start
  4.7 1.9 copy-start.1
  4.9 2.7 copy-start.2
  294.3 2.2 copy-start.5
  294.3 3.1 %copy-start.3 = (bf16[184,1440]{1,0:T(8,128)(2,1)S(1)}, bf16[184,1440]{1,0:T(8,128)(2,1)}, u32[]{:S(2)}) copy-start(bf16[184,1440]{1,0:T(8,128)(2,1)} %get-tuple-element.26) | copy-start | bytes 1589764
  294.4 3.0 %copy-start.4 = (bf16[184,1440]{1,0:T(8,128)(2,1)S(1)}, bf16[184,1440]{1,0:T(8,128)(2,1)}, u32[]{:S(2)}) copy-start(bf16[184,1440]{1,0:T(8,128)(2,1)} %get-tuple-element.27) | copy-start | bytes 1589764

commit v2 on v1

v2 whole, which is shorter than its diff:
```python
import functools

import jax
import jax.numpy as jnp
from jax import lax
from jax.experimental import pallas as pl
from jax.experimental.pallas import tpu as pltpu
from jax.sharding import PartitionSpec as P

MESH = pl.DeviceIdType.MESH
SWISH_SLOPE = 1.702
F32, BF16 = jnp.float32, jnp.bfloat16
TOK = 128
CAP = 512
SLOT = 24
D = 1440
FH = 1440
OWN = 180
SENT = 184
CHUNK = 192
DP = 8 * CHUNK
PAIR = 2 * CHUNK
HALF = 96
SLOTS = 32 * SLOT
PLANE = 16 * SLOT
VM = functools.partial(pl.BlockSpec, memory_space=pltpu.VMEM)


def mul(value, k):
    return pl.multiple_of(value, k)


class Place:
    def __init__(self):
        e, d = lax.axis_index("expert"), lax.axis_index("dp")
        self.x, self.zl, self.y = e // 8, (e // 4) % 2, e % 4
        self.h, self.c = d // 2, d % 2
        self.e, self.d = e, d
        self.sibling = (e, self.h * 2 + 1 - self.c)
        self.up = (e, ((self.h + 1) % 4) * 2 + self.c)
        self.down = (e, ((self.h + 3) % 4) * 2 + self.c)
        self.partner = (self.x * 8 + (1 - self.zl) * 4 + self.y, d)
        self.p = self.x * 4 + self.y

    def plane(self, i, sign):
        px = (self.x + sign * (i // 4) + 4) % 4
        py = (self.y + sign * (i % 4) + 4) % 4
        return px * 4 + py, px, py

    def plane_device(self, px, py):
        return (px * 8 + self.zl * 4 + py, self.d)

    def block(self, px, py, bi):
        zb = self.zl if bi == 0 else 1 - self.zl
        return px * 8 + zb * 4 + py

    def greet(self):
        barrier = pltpu.get_barrier_semaphore()
        for peer in (self.sibling, self.up, self.down, self.partner):
            pl.semaphore_signal(barrier, inc=1, device_id=peer, device_id_type=MESH)

        @pl.loop(1, 16)
        def _(i):
            _, px, py = self.plane(i, 1)
            pl.semaphore_signal(
                barrier, inc=1, device_id=self.plane_device(px, py), device_id_type=MESH
            )

        pl.semaphore_wait(barrier, 19)


def remote(src, dst, ssem, rsem, device):
    return pltpu.make_async_remote_copy(
        src_ref=src, dst_ref=dst, send_sem=ssem, recv_sem=rsem, device_id=device, device_id_type=MESH
    )


def rows_of(block, size=SLOT):
    return pl.ds(mul(block * SLOT, 8), size)


def dot(a, b):
    return jnp.dot(a, b, preferred_element_type=F32)


def dot_nt(a, b):
    return lax.dot_general(a, b, (((1,), (1,)), ((), ())), preferred_element_type=F32)


def dot_tn(a, b):
    return lax.dot_general(a, b, (((0,), (0,)), ((), ())), preferred_element_type=F32)


def one_zero(flag):
    return jnp.where(flag, 1.0, 0.0)


def step_kernel(
    ids, gates_in, tok_in, cot_in, wg_in, wu_in, wd_in,
    gg_out, gu_out, gd_out, mixed_out,
    wg, wu, wd, meta, zmeta, tok, cot, ztok, zcot, send_x, send_g, recv_x, recv_g,
    x, g, hid, eo, acc_g, acc_u, acc_d, pd, ra_d, hr, fr, rets, rr, r_mat, mt, zsend, zrecv,
    loc_sem, zs, zr, ags, agr, dss, dsr, d2s, d2r, hss, hsr, fss, fsr, rs, rr_sem,
):
    me = Place()
    h, c = me.h, me.c
    weights = (wg, wu, wd)
    outs = (gd_out, gg_out, gu_out)
    dg, du = send_x.at[pl.ds(0, CAP), :], send_g.at[pl.ds(0, CAP), :]

    def up_j(k):
        return (h + k) % 4

    def base(j, core):
        return CHUNK * (2 * j + core)

    def rows_at(j, core, lo=0, size=SENT):
        return pl.ds(mul(base(j, core) + lo, 8), size)

    def shard(w, j, core, lo=0, size=SENT):
        return w.at[rows_at(j, core, lo, size), :]

    staged = (gg_out, gu_out, gd_out)
    own_copies = [
        pltpu.make_async_copy(src.at[0], dst, loc_sem.at[a])
        for a, (src, dst) in enumerate(zip((wg_in, wu_in, wd_in), staged))
    ]
    for cp in own_copies:
        cp.start()
    meta[0:4, :] = ids[...].astype(F32)
    meta[4:8, :] = gates_in[...]
    for ext, src in ((tok, tok_in), (cot, cot_in)):
        for k in range(8):
            ext[CHUNK * k : CHUNK * k + OWN, :] = src[OWN * k : OWN * (k + 1), :]
            live = lax.broadcasted_iota(jnp.int32, (CHUNK - OWN, TOK), 0) == 0
            flag = one_zero(live) if ext is tok and k == 0 else jnp.zeros((CHUNK - OWN, TOK), F32)
            ext[CHUNK * k + OWN : CHUNK * (k + 1), :] = flag.astype(BF16)
    for a, w in enumerate(weights):
        for k in range(8):
            w[pl.ds(CHUNK * k + SENT, CHUNK - SENT), :] = jnp.zeros((CHUNK - SENT, DP), BF16)
        own_copies[a].wait()
        w[rows_at(h, c), FH - 32 :] = jnp.zeros((SENT, DP - FH + 32), BF16)
        w[rows_at(h, c, SENT - 8, 8), :] = jnp.zeros((8, DP), BF16)
        w[rows_at(h, c, 0, OWN), :FH] = staged[a][...]

    me.greet()

    zex = [
        remote(src, dst, zs.at[k], zr.at[k], me.partner)
        for k, (src, dst) in enumerate(((meta, zmeta), (tok, ztok), (cot, zcot)))
    ]
    for cp in zex:
        cp.start()

    def ag(a, k):
        w = weights[a]
        s, r = ags.at[a * 9 + k], agr.at[a * 9 + k]
        if k == 0:
            return remote(shard(w, h, c), shard(w, h, c), s, r, me.up)
        if k == 1:
            return remote(shard(w, h, c), shard(w, h, c), s, r, me.down)
        if k == 2:
            return remote(shard(w, h, c), shard(w, h, c), s, r, me.sibling)
        if k == 3:
            part = shard(w, up_j(3), c, 0, HALF)
            return remote(part, part, s, r, me.up)
        if k == 4:
            part = shard(w, up_j(1), c, HALF, SENT - HALF)
            return remote(part, part, s, r, me.down)
        if k in (5, 6):
            part = shard(w, up_j(3 if k == 5 else 1), c)
            return remote(part, part, s, r, me.sibling)
        part = shard(w, up_j(2), c, 0, HALF) if k == 7 else shard(w, up_j(2), c, HALF, SENT - HALF)
        return remote(part, part, s, r, me.sibling)

    def ag_in(a, k):
        w = weights[a]
        s, r = ags.at[a * 9 + k], agr.at[a * 9 + k]
        lo, size = 0, SENT
        if k == 0:
            j, core = up_j(3), c
        elif k == 1:
            j, core = up_j(1), c
        elif k == 2:
            j, core = h, 1 - c
        elif k == 3:
            j, core, size = up_j(2), c, HALF
        elif k == 4:
            j, core, lo, size = up_j(2), c, HALF, SENT - HALF
        elif k in (5, 6):
            j, core = up_j(3 if k == 5 else 1), 1 - c
        elif k == 7:
            j, core, size = up_j(2), 1 - c, HALF
        else:
            j, core, lo, size = up_j(2), 1 - c, HALF, SENT - HALF
        part = shard(w, j, core, lo, size)
        return remote(part, part, s, r, me.sibling)

    for a in (0, 1):
        for k in (0, 1, 2):
            ag(a, k).start()

    def dispatch_copy(bi, i, incoming):
        p, px, py = me.plane(i, -1 if incoming else 1)
        at = (bi * 16 + p) * SLOT
        source = me.block(px, py, bi) if incoming else me.block(me.x, me.y, bi)
        copies = []
        for arr, (src, dst) in enumerate(((send_x, recv_x), (send_g, recv_g))):
            k = (bi * 2 + arr) * 16 + i
            copies.append(
                remote(
                    src.at[pl.ds(mul(at, 8), SLOT), :],
                    dst.at[rows_of(source), :],
                    dss.at[k],
                    dsr.at[k],
                    me.plane_device(px, py),
                )
            )
        return copies

    def dispatch(bi, m_ref, t_ref, c_ref):
        place = lax.broadcasted_iota(jnp.int32, (16, TOK), 0)
        expert = ((place // 4) * 8 + me.zl * 4 + place % 4).astype(F32)
        named = jnp.zeros((16, TOK), F32)
        gates = jnp.zeros((16, TOK), F32)
        for k in range(4):
            hit = m_ref[k : k + 1, :] == expert
            named = named + one_zero(hit)
            gates = gates + jnp.where(hit, m_ref[4 + k : 5 + k, :], 0.0)
        earlier = one_zero(
            lax.broadcasted_iota(jnp.int32, (TOK, TOK), 0) < lax.broadcasted_iota(jnp.int32, (TOK, TOK), 1)
        ).astype(BF16)
        rank = dot(named.astype(BF16), earlier)
        rank = jnp.where(named > 0.5, rank, -1.0)
        slot = lax.broadcasted_iota(jnp.int32, (16, SLOT, TOK), 1).astype(F32)
        chosen3 = one_zero(slot == rank[:, None, :])
        weighted = (chosen3 * gates[:, None, :]).reshape(PLANE, TOK)
        pick = chosen3.reshape(PLANE, TOK).astype(BF16)
        mt[bi] = weighted
        slot_gate = jnp.sum(weighted, axis=1, keepdims=True)
        send_x[pl.ds(bi * PLANE, PLANE), :] = dot_nt(pick, t_ref[...]).astype(BF16)
        send_g[pl.ds(bi * PLANE, PLANE), :] = (dot_nt(pick, c_ref[...]) * slot_gate).astype(BF16)
        mine = rows_of(me.block(me.x, me.y, bi))
        here = pl.ds(mul((bi * 16 + me.p) * SLOT, 8), SLOT)
        recv_x[mine, :] = send_x[here, :]
        recv_g[mine, :] = send_g[here, :]

        @pl.loop(1, 16)
        def _(i):
            for cp in dispatch_copy(bi, i, False):
                cp.start()

    dispatch(0, meta, tok, cot)
    for cp in zex:
        cp.wait_recv()
    dispatch(1, zmeta, ztok, zcot)

    def forward_neighbours(a):
        ag_in(a, 0).wait_recv()
        ag(a, 3).start()
        ag(a, 5).start()
        ag_in(a, 1).wait_recv()
        ag(a, 4).start()
        ag(a, 6).start()

    forward_neighbours(0)
    forward_neighbours(1)
    for k in (0, 1, 2):
        ag(2, k).start()

    for bi in range(2):

        @pl.loop(1, 16)
        def _(i):
            for cp in dispatch_copy(bi, i, True):
                cp.wait_recv()

    eye_lane = one_zero(lax.broadcasted_iota(jnp.int32, (8, 128), 1) == OWN - 128).astype(BF16)
    flags = dot_nt(eye_lane, recv_x[:, 128:256])
    before = one_zero(
        lax.broadcasted_iota(jnp.int32, (SLOTS, SLOTS), 0) < lax.broadcasted_iota(jnp.int32, (SLOTS, SLOTS), 1)
    ).astype(BF16)
    position = dot(flags.astype(BF16), before)
    position = jnp.where(flags > 0.5, position, -1.0)[0:1, :]

    @pl.loop(0, 2)
    def _(m):
        at = mul(m * 256, 256)
        row = (lax.broadcasted_iota(jnp.int32, (256, SLOTS), 0) + at).astype(F32)
        pick = one_zero(row == position).astype(BF16)
        r_mat[pl.ds(at, 256), :] = pick
        x[pl.ds(at, 256), :] = dot(pick, recv_x[...]).astype(BF16)
        g[pl.ds(at, 256), :] = dot(pick, recv_g[...]).astype(BF16)

    def project(j, first):
        cols = pl.ds(mul(j * PAIR, 128), PAIR)

        @pl.loop(0, 2)
        def _(m):
            rows = pl.ds(mul(m * 256, 256), 256)
            xs = x[rows, cols]
            for acc, w in ((acc_g, wg), (acc_u, wu)):
                part = dot(xs, w[cols, :])
                acc[rows, :] = part if first else acc[rows, :] + part

    for a in (0, 1):
        ag_in(a, 2).wait_recv()
    project(h, True)
    for a in (0, 1):
        ag_in(a, 5).wait_recv()
    project(up_j(3), False)
    for a in (0, 1):
        ag_in(a, 6).wait_recv()
    project(up_j(1), False)

    def finish_gather(a):
        ag_in(a, 3).wait_recv()
        ag(a, 7).start()
        ag_in(a, 4).wait_recv()
        ag(a, 8).start()

    def wait_opposite(a):
        ag_in(a, 7).wait_recv()
        ag_in(a, 8).wait_recv()

    finish_gather(0)
    finish_gather(1)
    wait_opposite(0)
    wait_opposite(1)
    project(up_j(2), False)

    @pl.loop(0, 16)
    def _(m):
        rows = pl.ds(mul(m * 32, 32), 32)
        gate, up = acc_g[rows, :], acc_u[rows, :] + 1.0
        sg = jax.nn.sigmoid(SWISH_SLOPE * gate)
        value = gate * sg
        slope = sg + SWISH_SLOPE * value * (1.0 - sg)
        hid[rows, :] = (value * up).astype(BF16)
        acc_g[rows, :] = up * slope
        acc_u[rows, :] = value

    arrays = ((pd, g, hid), (wg, x, dg), (wu, x, du))

    def ra(a, k):
        if a == 0:
            return ra_d.at[k]
        return (recv_x, recv_g)[a - 1].at[pl.ds(CHUNK * k, SENT), :]

    def exchange(a, k):
        return remote(
            shard(arrays[a][0], up_j(k), 1 - c), ra(a, k), d2s.at[a * 4 + k], d2r.at[a * 4 + k], me.sibling
        )

    def parts_of(a):
        parts, left, right = arrays[a]
        for k in (2, 1, 3, 0):
            cols = pl.ds(mul(up_j(k) * PAIR, 128), PAIR)
            parts[cols, :] = dot_tn(left[:, cols], right[...]).astype(BF16)
            exchange(a, k).start()

    def half(a, k):
        lo, size = ((0, HALF), (HALF, SENT - HALF))[k]
        return remote(
            shard(arrays[a][0], up_j(2), c, lo, size),
            hr.at[a, pl.ds(lo, size), :],
            hss.at[a * 2 + k],
            hsr.at[a * 2 + k],
            (me.up, me.down)[k],
        )

    def full(a, k):
        return remote(
            shard(arrays[a][0], up_j((1, 3)[k]), c),
            fr.at[a * 2 + k],
            fss.at[a * 2 + k],
            fsr.at[a * 2 + k],
            (me.up, me.down)[k],
        )

    def send_halves(a):
        exchange(a, 2).wait_recv()
        rows = rows_at(up_j(2), c)
        parts = arrays[a][0]
        parts[rows, :] = (parts[rows, :].astype(F32) + ra(a, 2)[...].astype(F32)).astype(BF16)
        half(a, 0).start()
        half(a, 1).start()

    def send_fulls(a):
        parts = arrays[a][0]
        for k, jj in ((0, 1), (1, 3)):
            exchange(a, jj).wait_recv()
            half(a, k).wait_recv()
            for with_half in (True, False):
                lo, size = ((0, HALF), (HALF, SENT - HALF))[k if with_half else 1 - k]
                rows = rows_at(up_j(jj), c, lo, size)
                total = parts[rows, :].astype(F32) + ra(a, jj)[lo : lo + size, :].astype(F32)
                if with_half:
                    total = total + hr[a, pl.ds(lo, size), :].astype(F32)
                parts[rows, :] = total.astype(BF16)
            full(a, k).start()

    def down_step(j, first):
        cols = pl.ds(mul(j * PAIR, 128), PAIR)

        @pl.loop(0, 2)
        def _(m):
            rows = pl.ds(mul(m * 256, 256), 256)
            part = dot(g[rows, cols], wd[cols, :])
            acc_d[rows, :] = part if first else acc_d[rows, :] + part

    def out_step(j):
        cols = pl.ds(mul(j * PAIR, 128), PAIR)

        @pl.loop(0, 2)
        def _(m):
            rows = pl.ds(mul(m * 256, 256), 256)
            eo[rows, cols] = dot_nt(hid[rows, :], wd[cols, :]).astype(BF16)

    parts_of(0)
    for cp in zex:
        cp.wait_send()
    for bi in range(2):

        @pl.loop(1, 16)
        def _(i):
            for cp in dispatch_copy(bi, i, False):
                cp.wait_send()

    for a in range(2):
        for k in range(9):
            ag(a, k).wait_send()
    forward_neighbours(2)
    send_halves(0)
    ag_in(2, 2).wait_recv()
    down_step(h, True)
    out_step(h)
    ag_in(2, 5).wait_recv()
    down_step(up_j(3), False)
    ag_in(2, 6).wait_recv()
    down_step(up_j(1), False)
    finish_gather(2)
    wait_opposite(2)
    down_step(up_j(2), False)

    @pl.loop(0, 16)
    def _(m):
        rows = pl.ds(mul(m * 32, 32), 32)
        dh = acc_d[rows, :]
        dg[rows, :] = (dh * acc_g[rows, :]).astype(BF16)
        du[rows, :] = (dh * acc_u[rows, :]).astype(BF16)

    parts_of(1)
    send_halves(1)
    send_fulls(0)
    parts_of(2)
    send_halves(2)
    for k in (3, 1, 2):
        out_step(up_j(k))

    def back_copy(bi, i, incoming):
        p, px, py = me.plane(i, -1 if incoming else 1)
        place = p if incoming else me.p
        k = bi * 16 + i
        return remote(
            rets.at[rows_of(me.block(px, py, bi)), :],
            rr.at[pl.ds(mul((bi * 16 + place) * SLOT, 8), SLOT), :],
            rs.at[k],
            rr_sem.at[k],
            me.plane_device(px, py),
        )

    @pl.loop(0, 2)
    def _(m):
        cols = pl.ds(mul(m * PLANE, 128), PLANE)
        rets[pl.ds(mul(m * PLANE, 8), PLANE), :] = dot_tn(r_mat[:, cols], eo[...]).astype(BF16)

    for bi in range(2):
        rr[pl.ds(mul((bi * 16 + me.p) * SLOT, 8), SLOT), :] = rets[rows_of(me.block(me.x, me.y, bi)), :]

        @pl.loop(1, 16)
        def _(i):
            back_copy(bi, i, False).start()

    send_fulls(1)

    for bi in range(2):

        @pl.loop(1, 16)
        def _(i):
            back_copy(bi, i, True).wait_recv()

    def combine(bi):
        weight = mt[bi]
        high = weight.astype(BF16)
        low = (weight - high.astype(F32)).astype(BF16)
        both = dot_tn(rr[pl.ds(bi * PLANE, PLANE), :], jnp.concatenate([high, low], axis=1))
        return both[:, :TOK] + both[:, TOK:]

    zsend[...] = combine(1).astype(BF16)
    zcopy = remote(zsend, zrecv, zs.at[3], zr.at[3], me.partner)
    zcopy.start()
    send_fulls(2)
    own = combine(0)
    zcopy.wait_recv()
    mixed = (own + zrecv[...].astype(F32)).astype(BF16)
    for k in range(8):
        mixed_out[OWN * k : OWN * (k + 1), :] = mixed[CHUNK * k : CHUNK * k + OWN, :]

    for a in range(3):
        exchange(a, 0).wait_recv()
        total = arrays[a][0][rows_at(h, c), :].astype(F32) + ra(a, 0)[...].astype(F32)
        for k in range(2):
            full(a, k).wait_recv()
            total = total + fr[a * 2 + k].astype(F32)
        outs[a][...] = total.astype(BF16)[:OWN, :FH]

    zcopy.wait_send()
    for k in range(9):
        ag(2, k).wait_send()
    for a in range(3):
        for k in range(4):
            exchange(a, k).wait_send()
        for k in range(2):
            half(a, k).wait_send()
            full(a, k).wait_send()
    for bi in range(2):

        @pl.loop(1, 16)
        def _(i):
            back_copy(bi, i, False).wait_send()


def body(tokens, cotangent, expert_ids, gate_weights, w_gate, w_up, w_down):
    dma = pltpu.SemaphoreType.DMA
    b16 = lambda *shape: pltpu.VMEM(shape, BF16)
    f32 = lambda *shape: pltpu.VMEM(shape, F32)
    gg, gu, gd, mixed = pl.pallas_call(
        step_kernel,
        name="step",
        out_shape=[jax.ShapeDtypeStruct((OWN, FH), BF16)] * 3 + [jax.ShapeDtypeStruct((D, TOK), BF16)],
        in_specs=[VM()] * 4 + [pl.BlockSpec(memory_space=pl.ANY)] * 3,
        out_specs=[VM()] * 4,
        scratch_shapes=[
            b16(DP, DP), b16(DP, DP), b16(DP, DP),
            f32(8, TOK), f32(8, TOK), b16(DP, TOK), b16(DP, TOK), b16(DP, TOK), b16(DP, TOK),
            b16(SLOTS, DP), b16(SLOTS, DP), b16(SLOTS, DP), b16(SLOTS, DP),
            b16(CAP, DP), b16(CAP, DP), b16(CAP, DP), b16(CAP, DP),
            f32(CAP, DP), f32(CAP, DP), f32(CAP, DP),
            b16(DP, DP), b16(4, SENT, DP), b16(3, SENT, DP), b16(6, SENT, DP),
            b16(SLOTS, DP), b16(SLOTS, DP), b16(CAP, SLOTS), f32(2, PLANE, TOK), b16(DP, TOK), b16(DP, TOK),
            dma((3,)), dma((4,)), dma((4,)), dma((27,)), dma((27,)), dma((64,)), dma((64,)),
            dma((12,)), dma((12,)), dma((6,)), dma((6,)), dma((6,)), dma((6,)), dma((32,)), dma((32,)),
        ],
        compiler_params=pltpu.CompilerParams(
            collective_id=0, has_side_effects=True, vmem_limit_bytes=67043328
        ),
    )(expert_ids.T, gate_weights.T, tokens.T, cotangent.T, w_gate, w_up, w_down)
    return mixed.T, gg[None], gu[None], gd[None]


def solution(mesh):
    rows, weight = P(("expert", "dp"), None), P("expert", "dp", None)
    return jax.shard_map(
        body,
        mesh=mesh,
        in_specs=(rows, rows, rows, rows, weight, weight, weight),
        out_specs=(rows, weight, weight, weight),
        check_vma=False,
    )
```

time: 299 us -> 275 us (0.920)
  the two profiles are of different devices: /device:TPU:56 before, /device:TPU:1 now
where the time goes in v2:
time: 275 us; the launch traced here: 274 us
  Pallas kernels  269 us (98%)
  local copies, waits for them, and re-layouts  5.14 us (2%)
    pallas_call x1, Pallas kernels, body(): pl.pallas_call(step_kernel, name='step', out_shape=[jax.ShapeDtypeStruct(...  269 us

profile of v2, /device:TPU:1, one launch (start us, length us, event | category | flops | bytes accessed | tf_op | source)
XLA Modules:
  0.0 274.5 jit_solution(7075731053732044282)
XLA Ops:
  0.6 268.7 %step.1 = (bf16[180,1440]{1,0:T(8,128)(2,1)}, bf16[180,1440]{1,0:T(8,128)(2,1)}, bf16[180,1440]{1,0:T(8,128)(2,1)}, bf16[1440,128]{1,0:T(8,128)(2,1)}) custom-call(s32[4,128]{1,0:T(4,128)} %bitcast.14, f32[4,128]{1,0:T(4,128)} %bitcast.15, bf16[1440,128]{1,0:T(8,128)(2,1)} %bitcast.11, bf16[1440,128]{1,0:T(8,128)(2,1)} %bitcast.12, ...), custom_call_target="tpu_custom_call" | custom-call | tf_op jit(solution)/shard_map/step/pallas_call | solution.py:538
  269.3 0.0 copy-start.2
  269.3 1.8 copy.15
  271.1 0.0 copy-done.2
  271.1 0.0 copy-start.1
  271.2 0.8 copy.16
  272.0 0.5 copy-done.1
  272.4 0.0 copy-start
  272.4 0.8 copy.17
  273.2 0.5 copy-done
  273.7 0.8 copy.18
Async XLA Ops:
  269.3 1.8 copy-start.2
  271.1 1.3 copy-start.1
  272.4 1.3 copy-start

commit v3 on v2

--- a/solution.py
+++ b/solution.py
@@ -20,6 +20,8 @@
 CHUNK = 192
 DP = 8 * CHUNK
 PAIR = 2 * CHUNK
+MAIN = 1408
+REST = FH - MAIN
 HALF = 96
 SLOTS = 32 * SLOT
 PLANE = 16 * SLOT
@@ -98,13 +100,13 @@
 def step_kernel(
     ids, gates_in, tok_in, cot_in, wg_in, wu_in, wd_in,
     gg_out, gu_out, gd_out, mixed_out,
-    wg, wu, wd, meta, zmeta, tok, cot, ztok, zcot, send_x, send_g, recv_x, recv_g,
+    wg, wu, wd, wrem, grem, ra_rem, hr_rem, fr_rem, meta, zmeta, tok, cot, ztok, zcot, send_x, send_g, recv_x, recv_g,
     x, g, hid, eo, acc_g, acc_u, acc_d, pd, ra_d, hr, fr, rets, rr, r_mat, mt, zsend, zrecv,
     loc_sem, zs, zr, ags, agr, dss, dsr, d2s, d2r, hss, hsr, fss, fsr, rs, rr_sem,
 ):
     me = Place()
     h, c = me.h, me.c
-    weights = (wg, wu, wd)
+    weights = (wg, wu, wd, wrem)
     outs = (gd_out, gg_out, gu_out)
     dg, du = send_x.at[pl.ds(0, CAP), :], send_g.at[pl.ds(0, CAP), :]
 
@@ -117,8 +119,11 @@
     def rows_at(j, core, lo=0, size=SENT):
         return pl.ds(mul(base(j, core) + lo, 8), size)
 
-    def shard(w, j, core, lo=0, size=SENT):
-        return w.at[rows_at(j, core, lo, size), :]
+    def width(a):
+        return pl.ds(0, MAIN if a < 3 else 128)
+
+    def shard(a, w, j, core, lo=0, size=SENT):
+        return w.at[rows_at(j, core, lo, size), width(a)]
 
     staged = (gg_out, gu_out, gd_out)
     own_copies = [
@@ -136,12 +141,16 @@
             flag = one_zero(live) if ext is tok and k == 0 else jnp.zeros((CHUNK - OWN, TOK), F32)
             ext[CHUNK * k + OWN : CHUNK * (k + 1), :] = flag.astype(BF16)
     for a, w in enumerate(weights):
+        lanes = w.shape[1]
         for k in range(8):
-            w[pl.ds(CHUNK * k + SENT, CHUNK - SENT), :] = jnp.zeros((CHUNK - SENT, DP), BF16)
-        own_copies[a].wait()
-        w[rows_at(h, c), FH - 32 :] = jnp.zeros((SENT, DP - FH + 32), BF16)
-        w[rows_at(h, c, SENT - 8, 8), :] = jnp.zeros((8, DP), BF16)
-        w[rows_at(h, c, 0, OWN), :FH] = staged[a][...]
+            w[pl.ds(CHUNK * k + SENT, CHUNK - SENT), :] = jnp.zeros((CHUNK - SENT, lanes), BF16)
+        w[rows_at(h, c, SENT - 8, 8), :] = jnp.zeros((8, lanes), BF16)
+        if a < 3:
+            own_copies[a].wait()
+            w[rows_at(h, c, 0, OWN), :MAIN] = staged[a][:, :MAIN]
+    wrem[rows_at(h, c, 0, OWN), :] = jnp.concatenate(
+        [ref[:, MAIN:] for ref in staged] + [jnp.zeros((OWN, 128 - 3 * REST), BF16)], axis=1
+    )
 
     me.greet()
 
@@ -156,21 +165,21 @@
         w = weights[a]
         s, r = ags.at[a * 9 + k], agr.at[a * 9 + k]
         if k == 0:
-            return remote(shard(w, h, c), shard(w, h, c), s, r, me.up)
+            return remote(shard(a, w, h, c), shard(a, w, h, c), s, r, me.up)
         if k == 1:
-            return remote(shard(w, h, c), shard(w, h, c), s, r, me.down)
+            return remote(shard(a, w, h, c), shard(a, w, h, c), s, r, me.down)
         if k == 2:
-            return remote(shard(w, h, c), shard(w, h, c), s, r, me.sibling)
+            return remote(shard(a, w, h, c), shard(a, w, h, c), s, r, me.sibling)
         if k == 3:
-            part = shard(w, up_j(3), c, 0, HALF)
+            part = shard(a, w, up_j(3), c, 0, HALF)
             return remote(part, part, s, r, me.up)
         if k == 4:
-            part = shard(w, up_j(1), c, HALF, SENT - HALF)
+            part = shard(a, w, up_j(1), c, HALF, SENT - HALF)
             return remote(part, part, s, r, me.down)
         if k in (5, 6):
-            part = shard(w, up_j(3 if k == 5 else 1), c)
+            part = shard(a, w, up_j(3 if k == 5 else 1), c)
             return remote(part, part, s, r, me.sibling)
-        part = shard(w, up_j(2), c, 0, HALF) if k == 7 else shard(w, up_j(2), c, HALF, SENT - HALF)
+        part = shard(a, w, up_j(2), c, 0, HALF) if k == 7 else shard(a, w, up_j(2), c, HALF, SENT - HALF)
         return remote(part, part, s, r, me.sibling)
 
     def ag_in(a, k):
@@ -193,10 +202,10 @@
             j, core, size = up_j(2), 1 - c, HALF
         else:
             j, core, lo, size = up_j(2), 1 - c, HALF, SENT - HALF
-        part = shard(w, j, core, lo, size)
+        part = shard(a, w, j, core, lo, size)
         return remote(part, part, s, r, me.sibling)
 
-    for a in (0, 1):
+    for a in (3, 0, 1):
         for k in (0, 1, 2):
             ag(a, k).start()
 
@@ -263,6 +272,7 @@
         ag(a, 4).start()
         ag(a, 6).start()
 
+    forward_neighbours(3)
     forward_neighbours(0)
     forward_neighbours(1)
     for k in (0, 1, 2):
@@ -294,6 +304,11 @@
 
     def project(j, first):
         cols = pl.ds(mul(j * PAIR, 128), PAIR)
+        rest = wrem[cols, :].astype(F32)
+        lane = lax.broadcasted_iota(jnp.int32, (PAIR, 128), 1)
+        for a in range(3):
+            own = rest if a == 0 else pltpu.roll(rest, 128 - REST * a, 1)
+            weights[a][cols, MAIN:] = jnp.where(lane < REST, own, 0.0).astype(BF16)
 
         @pl.loop(0, 2)
         def _(m):
@@ -303,13 +318,13 @@
                 part = dot(xs, w[cols, :])
                 acc[rows, :] = part if first else acc[rows, :] + part
 
-    for a in (0, 1):
+    for a in (3, 0, 1):
         ag_in(a, 2).wait_recv()
     project(h, True)
-    for a in (0, 1):
+    for a in (3, 0, 1):
         ag_in(a, 5).wait_recv()
     project(up_j(3), False)
-    for a in (0, 1):
+    for a in (3, 0, 1):
         ag_in(a, 6).wait_recv()
     project(up_j(1), False)
 
@@ -323,10 +338,10 @@
         ag_in(a, 7).wait_recv()
         ag_in(a, 8).wait_recv()
 
-    finish_gather(0)
-    finish_gather(1)
-    wait_opposite(0)
-    wait_opposite(1)
+    for a in (3, 0, 1):
+        finish_gather(a)
+    for a in (3, 0, 1):
+        wait_opposite(a)
     project(up_j(2), False)
 
     @pl.loop(0, 16)
@@ -340,30 +355,43 @@
         acc_g[rows, :] = up * slope
         acc_u[rows, :] = value
 
-    arrays = ((pd, g, hid), (wg, x, dg), (wu, x, du))
+    arrays = ((pd, g, hid), (wg, x, dg), (wu, x, du), (grem, None, None))
 
     def ra(a, k):
-        if a == 0:
-            return ra_d.at[k]
-        return (recv_x, recv_g)[a - 1].at[pl.ds(CHUNK * k, SENT), :]
+        if a in (0, 3):
+            return (ra_d if a == 0 else ra_rem).at[k]
+        return (recv_x, recv_g)[a - 1].at[pl.ds(CHUNK * k, SENT), width(a)]
+
+    def half_in(a, lo, size):
+        return hr.at[a, pl.ds(lo, size), :] if a < 3 else hr_rem.at[pl.ds(lo, size), :]
+
+    def full_in(a, k):
+        return fr.at[a * 2 + k] if a < 3 else fr_rem.at[k]
 
     def exchange(a, k):
         return remote(
-            shard(arrays[a][0], up_j(k), 1 - c), ra(a, k), d2s.at[a * 4 + k], d2r.at[a * 4 + k], me.sibling
+            shard(a, arrays[a][0], up_j(k), 1 - c), ra(a, k), d2s.at[a * 4 + k], d2r.at[a * 4 + k], me.sibling
         )
 
-    def parts_of(a):
+    def parts_of(a, ks):
         parts, left, right = arrays[a]
-        for k in (2, 1, 3, 0):
+        for k in ks:
             cols = pl.ds(mul(up_j(k) * PAIR, 128), PAIR)
-            parts[cols, :] = dot_tn(left[:, cols], right[...]).astype(BF16)
+            part = dot_tn(left[:, cols], right[...])
+            parts[cols, :MAIN] = part[:, :MAIN].astype(BF16)
             exchange(a, k).start()
+            rest = part[:, MAIN:]
+            if a > 0:
+                rest = grem[cols, :].astype(F32) + pltpu.roll(rest, REST * a, 1)
+            grem[cols, :] = rest.astype(BF16)
+            if a == 2:
+                exchange(3, k).start()
 
     def half(a, k):
         lo, size = ((0, HALF), (HALF, SENT - HALF))[k]
         return remote(
-            shard(arrays[a][0], up_j(2), c, lo, size),
-            hr.at[a, pl.ds(lo, size), :],
+            shard(a, arrays[a][0], up_j(2), c, lo, size),
+            half_in(a, lo, size),
             hss.at[a * 2 + k],
             hsr.at[a * 2 + k],
             (me.up, me.down)[k],
@@ -371,8 +399,8 @@
 
     def full(a, k):
         return remote(
-            shard(arrays[a][0], up_j((1, 3)[k]), c),
-            fr.at[a * 2 + k],
+            shard(a, arrays[a][0], up_j((1, 3)[k]), c),
+            full_in(a, k),
             fss.at[a * 2 + k],
             fsr.at[a * 2 + k],
             (me.up, me.down)[k],
@@ -380,9 +408,9 @@
 
     def send_halves(a):
         exchange(a, 2).wait_recv()
-        rows = rows_at(up_j(2), c)
+        at = rows_at(up_j(2), c), width(a)
         parts = arrays[a][0]
-        parts[rows, :] = (parts[rows, :].astype(F32) + ra(a, 2)[...].astype(F32)).astype(BF16)
+        parts[at] = (parts[at].astype(F32) + ra(a, 2)[...].astype(F32)).astype(BF16)
         half(a, 0).start()
         half(a, 1).start()
 
@@ -393,11 +421,11 @@
             half(a, k).wait_recv()
             for with_half in (True, False):
                 lo, size = ((0, HALF), (HALF, SENT - HALF))[k if with_half else 1 - k]
-                rows = rows_at(up_j(jj), c, lo, size)
-                total = parts[rows, :].astype(F32) + ra(a, jj)[lo : lo + size, :].astype(F32)
+                at = rows_at(up_j(jj), c, lo, size), width(a)
+                total = parts[at].astype(F32) + ra(a, jj)[lo : lo + size, :].astype(F32)
                 if with_half:
-                    total = total + hr[a, pl.ds(lo, size), :].astype(F32)
-                parts[rows, :] = total.astype(BF16)
+                    total = total + half_in(a, lo, size)[...].astype(F32)
+                parts[at] = total.astype(BF16)
             full(a, k).start()
 
     def down_step(j, first):
@@ -417,7 +445,7 @@
             rows = pl.ds(mul(m * 256, 256), 256)
             eo[rows, cols] = dot_nt(hid[rows, :], wd[cols, :]).astype(BF16)
 
-    parts_of(0)
+    parts_of(0, (2, 1, 3, 0))
     for cp in zex:
         cp.wait_send()
     for bi in range(2):
@@ -427,7 +455,7 @@
             for cp in dispatch_copy(bi, i, False):
                 cp.wait_send()
 
-    for a in range(2):
+    for a in (3, 0, 1):
         for k in range(9):
             ag(a, k).wait_send()
     forward_neighbours(2)
@@ -450,11 +478,14 @@
         dg[rows, :] = (dh * acc_g[rows, :]).astype(BF16)
         du[rows, :] = (dh * acc_u[rows, :]).astype(BF16)
 
-    parts_of(1)
+    parts_of(1, (2, 1))
     send_halves(1)
     send_fulls(0)
-    parts_of(2)
+    parts_of(1, (3, 0))
+    parts_of(2, (2, 1))
     send_halves(2)
+    send_halves(3)
+    parts_of(2, (3, 0))
     for k in (3, 1, 2):
         out_step(up_j(k))
 
@@ -501,24 +532,30 @@
     zcopy = remote(zsend, zrecv, zs.at[3], zr.at[3], me.partner)
     zcopy.start()
     send_fulls(2)
+    send_fulls(3)
     own = combine(0)
     zcopy.wait_recv()
     mixed = (own + zrecv[...].astype(F32)).astype(BF16)
     for k in range(8):
         mixed_out[OWN * k : OWN * (k + 1), :] = mixed[CHUNK * k : CHUNK * k + OWN, :]
 
-    for a in range(3):
+    for a in range(4):
         exchange(a, 0).wait_recv()
-        total = arrays[a][0][rows_at(h, c), :].astype(F32) + ra(a, 0)[...].astype(F32)
+        total = arrays[a][0][rows_at(h, c), width(a)].astype(F32) + ra(a, 0)[...].astype(F32)
         for k in range(2):
             full(a, k).wait_recv()
-            total = total + fr[a * 2 + k].astype(F32)
-        outs[a][...] = total.astype(BF16)[:OWN, :FH]
+            total = total + full_in(a, k)[...].astype(F32)
+        if a < 3:
+            outs[a][:, :MAIN] = total.astype(BF16)[:OWN]
+        else:
+            for b in range(3):
+                own = total if b == 0 else pltpu.roll(total, 128 - REST * b, 1)
+                outs[b][:, MAIN:] = own.astype(BF16)[:OWN, :REST]
 
     zcopy.wait_send()
     for k in range(9):
         ag(2, k).wait_send()
-    for a in range(3):
+    for a in range(4):
         for k in range(4):
             exchange(a, k).wait_send()
         for k in range(2):
@@ -542,15 +579,16 @@
         in_specs=[VM()] * 4 + [pl.BlockSpec(memory_space=pl.ANY)] * 3,
         out_specs=[VM()] * 4,
         scratch_shapes=[
-            b16(DP, DP), b16(DP, DP), b16(DP, DP),
+            b16(DP, DP), b16(DP, DP), b16(DP, DP), b16(DP, 128), b16(DP, 128),
+            b16(4, SENT, 128), b16(SENT, 128), b16(2, SENT, 128),
             f32(8, TOK), f32(8, TOK), b16(DP, TOK), b16(DP, TOK), b16(DP, TOK), b16(DP, TOK),
             b16(SLOTS, DP), b16(SLOTS, DP), b16(SLOTS, DP), b16(SLOTS, DP),
             b16(CAP, DP), b16(CAP, DP), b16(CAP, DP), b16(CAP, DP),
             f32(CAP, DP), f32(CAP, DP), f32(CAP, DP),
-            b16(DP, DP), b16(4, SENT, DP), b16(3, SENT, DP), b16(6, SENT, DP),
+            b16(DP, DP), b16(4, SENT, MAIN), b16(3, SENT, MAIN), b16(6, SENT, MAIN),
             b16(SLOTS, DP), b16(SLOTS, DP), b16(CAP, SLOTS), f32(2, PLANE, TOK), b16(DP, TOK), b16(DP, TOK),
-            dma((3,)), dma((4,)), dma((4,)), dma((27,)), dma((27,)), dma((64,)), dma((64,)),
-            dma((12,)), dma((12,)), dma((6,)), dma((6,)), dma((6,)), dma((6,)), dma((32,)), dma((32,)),
+            dma((3,)), dma((4,)), dma((4,)), dma((36,)), dma((36,)), dma((64,)), dma((64,)),
+            dma((16,)), dma((16,)), dma((8,)), dma((8,)), dma((8,)), dma((8,)), dma((32,)), dma((32,)),
         ],
         compiler_params=pltpu.CompilerParams(
             collective_id=0, has_side_effects=True, vmem_limit_bytes=67043328

time: 275 us -> 264 us (0.960)
  the two profiles are of different devices: /device:TPU:1 before, /device:TPU:56 now
where the time goes in v3:
time: 264 us
  Pallas kernels  258 us (98%)
  local copies, waits for them, and re-layouts  5.14 us (2%)
    pallas_call x1, Pallas kernels, body(): pl.pallas_call(step_kernel, name='step', out_shape=[jax.ShapeDtypeStruct(...  258 us

profile of v3, /device:TPU:56, one launch (start us, length us, event | category | flops | bytes accessed | tf_op | source)
XLA Modules:
  0.0 263.9 jit_solution(11053016111483748945)
XLA Ops:
  0.6 258.1 %step.1 = (bf16[180,1440]{1,0:T(8,128)(2,1)}, bf16[180,1440]{1,0:T(8,128)(2,1)}, bf16[180,1440]{1,0:T(8,128)(2,1)}, bf16[1440,128]{1,0:T(8,128)(2,1)}) custom-call(s32[4,128]{1,0:T(4,128)} %bitcast.14, f32[4,128]{1,0:T(4,128)} %bitcast.15, bf16[1440,128]{1,0:T(8,128)(2,1)} %bitcast.11, bf16[1440,128]{1,0:T(8,128)(2,1)} %bitcast.12, ...), custom_call_target="tpu_custom_call" | custom-call | tf_op jit(solution)/shard_map/step/pallas_call | solution.py:575
  258.8 0.0 copy-start.2
  258.8 1.8 copy.15
  260.6 0.0 copy-done.2
  260.6 0.0 copy-start.1
  260.6 0.8 copy.16
  261.4 0.5 copy-done.1
  261.8 0.0 copy-start
  261.8 0.8 copy.17
  262.6 0.5 copy-done
  263.1 0.8 copy.18
Async XLA Ops:
  258.8 1.8 copy-start.2
  260.6 1.3 copy-start.1
  261.8 1.3 copy-start

commit v4 on v3

--- a/solution.py
+++ b/solution.py
@@ -68,7 +68,8 @@
                 barrier, inc=1, device_id=self.plane_device(px, py), device_id_type=MESH
             )
 
-        pl.semaphore_wait(barrier, 19)
+    def await_greetings(self):
+        pl.semaphore_wait(pltpu.get_barrier_semaphore(), 19)
 
 
 def remote(src, dst, ssem, rsem, device):
@@ -105,6 +106,7 @@
     loc_sem, zs, zr, ags, agr, dss, dsr, d2s, d2r, hss, hsr, fss, fsr, rs, rr_sem,
 ):
     me = Place()
+    me.greet()
     h, c = me.h, me.c
     weights = (wg, wu, wd, wrem)
     outs = (gd_out, gg_out, gu_out)
@@ -134,12 +136,14 @@
         cp.start()
     meta[0:4, :] = ids[...].astype(F32)
     meta[4:8, :] = gates_in[...]
-    for ext, src in ((tok, tok_in), (cot, cot_in)):
+
+    def widen(ext, src, flagged):
         for k in range(8):
             ext[CHUNK * k : CHUNK * k + OWN, :] = src[OWN * k : OWN * (k + 1), :]
             live = lax.broadcasted_iota(jnp.int32, (CHUNK - OWN, TOK), 0) == 0
-            flag = one_zero(live) if ext is tok and k == 0 else jnp.zeros((CHUNK - OWN, TOK), F32)
+            flag = one_zero(live) if flagged and k == 0 else jnp.zeros((CHUNK - OWN, TOK), F32)
             ext[CHUNK * k + OWN : CHUNK * (k + 1), :] = flag.astype(BF16)
+
     for a, w in enumerate(weights):
         lanes = w.shape[1]
         for k in range(8):
@@ -152,11 +156,11 @@
         [ref[:, MAIN:] for ref in staged] + [jnp.zeros((OWN, 128 - 3 * REST), BF16)], axis=1
     )
 
-    me.greet()
+    me.await_greetings()
 
     zex = [
         remote(src, dst, zs.at[k], zr.at[k], me.partner)
-        for k, (src, dst) in enumerate(((meta, zmeta), (tok, ztok), (cot, zcot)))
+        for k, (src, dst) in enumerate(((meta, zmeta), (tok_in, ztok), (cot_in, zcot)))
     ]
     for cp in zex:
         cp.start()
@@ -259,10 +263,14 @@
             for cp in dispatch_copy(bi, i, False):
                 cp.start()
 
+    widen(tok, tok_in, True)
+    widen(cot, cot_in, False)
     dispatch(0, meta, tok, cot)
     for cp in zex:
         cp.wait_recv()
-    dispatch(1, zmeta, ztok, zcot)
+    widen(tok, ztok, True)
+    widen(cot, zcot, False)
+    dispatch(1, zmeta, tok, cot)
 
     def forward_neighbours(a):
         ag_in(a, 0).wait_recv()
@@ -458,8 +466,8 @@
     for a in (3, 0, 1):
         for k in range(9):
             ag(a, k).wait_send()
+    send_halves(0)
     forward_neighbours(2)
-    send_halves(0)
     ag_in(2, 2).wait_recv()
     down_step(h, True)
     out_step(h)
@@ -467,6 +475,7 @@
     down_step(up_j(3), False)
     ag_in(2, 6).wait_recv()
     down_step(up_j(1), False)
+    send_fulls(0)
     finish_gather(2)
     wait_opposite(2)
     down_step(up_j(2), False)
@@ -480,7 +489,6 @@
 
     parts_of(1, (2, 1))
     send_halves(1)
-    send_fulls(0)
     parts_of(1, (3, 0))
     parts_of(2, (2, 1))
     send_halves(2)
@@ -506,14 +514,13 @@
         cols = pl.ds(mul(m * PLANE, 128), PLANE)
         rets[pl.ds(mul(m * PLANE, 8), PLANE), :] = dot_tn(r_mat[:, cols], eo[...]).astype(BF16)
 
+    send_fulls(1)
     for bi in range(2):
         rr[pl.ds(mul((bi * 16 + me.p) * SLOT, 8), SLOT), :] = rets[rows_of(me.block(me.x, me.y, bi)), :]
 
         @pl.loop(1, 16)
         def _(i):
             back_copy(bi, i, False).start()
-
-    send_fulls(1)
 
     for bi in range(2):
 
@@ -528,16 +535,18 @@
         both = dot_tn(rr[pl.ds(bi * PLANE, PLANE), :], jnp.concatenate([high, low], axis=1))
         return both[:, :TOK] + both[:, TOK:]
 
-    zsend[...] = combine(1).astype(BF16)
+    theirs = combine(1).astype(BF16)
+    for k in range(8):
+        zsend[OWN * k : OWN * (k + 1), :] = theirs[CHUNK * k : CHUNK * k + OWN, :]
     zcopy = remote(zsend, zrecv, zs.at[3], zr.at[3], me.partner)
     zcopy.start()
     send_fulls(2)
     send_fulls(3)
     own = combine(0)
     zcopy.wait_recv()
-    mixed = (own + zrecv[...].astype(F32)).astype(BF16)
     for k in range(8):
-        mixed_out[OWN * k : OWN * (k + 1), :] = mixed[CHUNK * k : CHUNK * k + OWN, :]
+        at = slice(OWN * k, OWN * (k + 1))
+        mixed_out[at, :] = (own[CHUNK * k : CHUNK * k + OWN, :] + zrecv[at, :].astype(F32)).astype(BF16)
 
     for a in range(4):
         exchange(a, 0).wait_recv()
@@ -568,25 +577,40 @@
             back_copy(bi, i, False).wait_send()
 
 
+def copy_kernel(*refs):
+    srcs, dsts, held, (sem_in, sem_out) = refs[:4], refs[4:8], refs[8:12], refs[12:]
+    loads = [pltpu.make_async_copy(s, v, sem_in.at[i]) for i, (s, v) in enumerate(zip(srcs, held))]
+    stores = [pltpu.make_async_copy(v, d, sem_out.at[i]) for i, (v, d) in enumerate(zip(held, dsts))]
+    for load in loads:
+        load.start()
+    for load, store in zip(loads, stores):
+        load.wait()
+        store.start()
+    for store in stores:
+        store.wait()
+
+
 def body(tokens, cotangent, expert_ids, gate_weights, w_gate, w_up, w_down):
     dma = pltpu.SemaphoreType.DMA
     b16 = lambda *shape: pltpu.VMEM(shape, BF16)
     f32 = lambda *shape: pltpu.VMEM(shape, F32)
-    gg, gu, gd, mixed = pl.pallas_call(
+    results = [jax.ShapeDtypeStruct((OWN, FH), BF16)] * 3 + [jax.ShapeDtypeStruct((D, TOK), BF16)]
+    anywhere = pl.BlockSpec(memory_space=pl.ANY)
+    outs = pl.pallas_call(
         step_kernel,
         name="step",
-        out_shape=[jax.ShapeDtypeStruct((OWN, FH), BF16)] * 3 + [jax.ShapeDtypeStruct((D, TOK), BF16)],
-        in_specs=[VM()] * 4 + [pl.BlockSpec(memory_space=pl.ANY)] * 3,
+        out_shape=results,
+        in_specs=[VM()] * 4 + [anywhere] * 3,
         out_specs=[VM()] * 4,
         scratch_shapes=[
             b16(DP, DP), b16(DP, DP), b16(DP, DP), b16(DP, 128), b16(DP, 128),
             b16(4, SENT, 128), b16(SENT, 128), b16(2, SENT, 128),
-            f32(8, TOK), f32(8, TOK), b16(DP, TOK), b16(DP, TOK), b16(DP, TOK), b16(DP, TOK),
+            f32(8, TOK), f32(8, TOK), b16(DP, TOK), b16(DP, TOK), b16(D, TOK), b16(D, TOK),
             b16(SLOTS, DP), b16(SLOTS, DP), b16(SLOTS, DP), b16(SLOTS, DP),
             b16(CAP, DP), b16(CAP, DP), b16(CAP, DP), b16(CAP, DP),
             f32(CAP, DP), f32(CAP, DP), f32(CAP, DP),
             b16(DP, DP), b16(4, SENT, MAIN), b16(3, SENT, MAIN), b16(6, SENT, MAIN),
-            b16(SLOTS, DP), b16(SLOTS, DP), b16(CAP, SLOTS), f32(2, PLANE, TOK), b16(DP, TOK), b16(DP, TOK),
+            b16(SLOTS, DP), b16(SLOTS, DP), b16(CAP, SLOTS), f32(2, PLANE, TOK), b16(D, TOK), b16(D, TOK),
             dma((3,)), dma((4,)), dma((4,)), dma((36,)), dma((36,)), dma((64,)), dma((64,)),
             dma((16,)), dma((16,)), dma((8,)), dma((8,)), dma((8,)), dma((8,)), dma((32,)), dma((32,)),
         ],
@@ -594,6 +618,14 @@
             collective_id=0, has_side_effects=True, vmem_limit_bytes=67043328
         ),
     )(expert_ids.T, gate_weights.T, tokens.T, cotangent.T, w_gate, w_up, w_down)
+    gg, gu, gd, mixed = pl.pallas_call(
+        copy_kernel,
+        name="results",
+        out_shape=results,
+        in_specs=[anywhere] * 4,
+        out_specs=[anywhere] * 4,
+        scratch_shapes=[b16(*r.shape) for r in results] + [dma((4,)), dma((4,))],
+    )(*outs)
     return mixed.T, gg[None], gu[None], gd[None]
 
 

time: 264 us -> 258 us (0.977)
  local copies, waits for them, and re-layouts: 5.14 us -> 0 us
    unnamed x10 -> x0, local copies, waits for them, and re-layouts: 5.14 us -> none
    pallas_call x1 -> x2, Pallas kernels: 258 us -> 256 us  [the longest x1 253 us: body(): pl.pallas_call(step_kernel, name='step', out_shape=results, in_specs=[VM(...]
where the time goes in v4:
time: 258 us; the launch traced here: 256 us
  Pallas kernels  256 us (99%)
    pallas_call x1, Pallas kernels, body(): pl.pallas_call(step_kernel, name='step', out_shape=results, in_specs=[VM(...  253 us

profile of v4, /device:TPU:56, one launch (start us, length us, event | category | flops | bytes accessed | tf_op | source)
XLA Modules:
  0.0 256.5 jit_solution(10827264293083309935)
XLA Ops:
  0.6 253.3 %step.1 = (bf16[180,1440]{1,0:T(8,128)(2,1)}, bf16[180,1440]{1,0:T(8,128)(2,1)}, bf16[180,1440]{1,0:T(8,128)(2,1)}, bf16[1440,128]{1,0:T(8,128)(2,1)}) custom-call(s32[4,128]{1,0:T(4,128)} %bitcast.10, f32[4,128]{1,0:T(4,128)} %bitcast.11, bf16[1440,128]{1,0:T(8,128)(2,1)} %bitcast.8, bf16[1440,128]{1,0:T(8,128)(2,1)} %bitcast.9, ...), custom_call_target="tpu_custom_call" | custom-call | tf_op jit(solution)/shard_map/step/pallas_call | solution.py:599
  253.9 2.4 results.1

commit v5 on v4

--- a/solution.py
+++ b/solution.py
@@ -16,13 +16,17 @@
 D = 1440
 FH = 1440
 OWN = 180
-SENT = 184
+SENT = 176
+TAIL = OWN - SENT
 CHUNK = 192
 DP = 8 * CHUNK
 PAIR = 2 * CHUNK
 MAIN = 1408
 REST = FH - MAIN
-HALF = 96
+TILES = MAIN // 128
+MISC = OWN + 3 * TILES * TAIL
+MISC_HALF = 160
+HALF = 88
 SLOTS = 32 * SLOT
 PLANE = 16 * SLOT
 VM = functools.partial(pl.BlockSpec, memory_space=pltpu.VMEM)
@@ -121,11 +125,22 @@
     def rows_at(j, core, lo=0, size=SENT):
         return pl.ds(mul(base(j, core) + lo, 8), size)
 
+    def misc_at(j, core, lo=0, size=MISC):
+        return pl.ds(mul(MISC * (2 * j + core) + lo, 8), size)
+
+    def span(a, half=None):
+        rows, first = (SENT, HALF) if a < 3 else (MISC, MISC_HALF)
+        return (0, rows) if half is None else ((0, first), (first, rows - first))[half]
+
+    def place_of(a, j, core, half=None):
+        lo, size = span(a, half)
+        return (rows_at if a < 3 else misc_at)(j, core, lo, size), width(a)
+
     def width(a):
         return pl.ds(0, MAIN if a < 3 else 128)
 
-    def shard(a, w, j, core, lo=0, size=SENT):
-        return w.at[rows_at(j, core, lo, size), width(a)]
+    def shard(a, w, j, core, half=None):
+        return w.at[place_of(a, j, core, half)]
 
     staged = (gg_out, gu_out, gd_out)
     own_copies = [
@@ -144,17 +159,18 @@
             flag = one_zero(live) if flagged and k == 0 else jnp.zeros((CHUNK - OWN, TOK), F32)
             ext[CHUNK * k + OWN : CHUNK * (k + 1), :] = flag.astype(BF16)
 
-    for a, w in enumerate(weights):
-        lanes = w.shape[1]
+    for a, w in enumerate(weights[:3]):
         for k in range(8):
-            w[pl.ds(CHUNK * k + SENT, CHUNK - SENT), :] = jnp.zeros((CHUNK - SENT, lanes), BF16)
-        w[rows_at(h, c, SENT - 8, 8), :] = jnp.zeros((8, lanes), BF16)
-        if a < 3:
-            own_copies[a].wait()
-            w[rows_at(h, c, 0, OWN), :MAIN] = staged[a][:, :MAIN]
-    wrem[rows_at(h, c, 0, OWN), :] = jnp.concatenate(
-        [ref[:, MAIN:] for ref in staged] + [jnp.zeros((OWN, 128 - 3 * REST), BF16)], axis=1
+            w[pl.ds(CHUNK * k + SENT, CHUNK - SENT), :] = jnp.zeros((CHUNK - SENT, DP), BF16)
+        own_copies[a].wait()
+        w[rows_at(h, c), :MAIN] = staged[a][:SENT, :MAIN]
+    last_lanes = jnp.concatenate(
+        [ref[:, MAIN:].astype(F32) for ref in staged] + [jnp.zeros((OWN, 128 - 3 * REST), F32)], axis=1
     )
+    last_rows = [
+        ref[SENT:, 128 * t : 128 * (t + 1)].astype(F32) for ref in staged for t in range(TILES)
+    ]
+    wrem[misc_at(h, c), :] = jnp.concatenate([last_lanes, *last_rows], axis=0).astype(BF16)
 
     me.await_greetings()
 
@@ -175,38 +191,34 @@
         if k == 2:
             return remote(shard(a, w, h, c), shard(a, w, h, c), s, r, me.sibling)
         if k == 3:
-            part = shard(a, w, up_j(3), c, 0, HALF)
+            part = shard(a, w, up_j(3), c, 0)
             return remote(part, part, s, r, me.up)
         if k == 4:
-            part = shard(a, w, up_j(1), c, HALF, SENT - HALF)
+            part = shard(a, w, up_j(1), c, 1)
             return remote(part, part, s, r, me.down)
         if k in (5, 6):
             part = shard(a, w, up_j(3 if k == 5 else 1), c)
             return remote(part, part, s, r, me.sibling)
-        part = shard(a, w, up_j(2), c, 0, HALF) if k == 7 else shard(a, w, up_j(2), c, HALF, SENT - HALF)
+        part = shard(a, w, up_j(2), c, k - 7)
         return remote(part, part, s, r, me.sibling)
 
     def ag_in(a, k):
         w = weights[a]
         s, r = ags.at[a * 9 + k], agr.at[a * 9 + k]
-        lo, size = 0, SENT
+        half = None
         if k == 0:
             j, core = up_j(3), c
         elif k == 1:
             j, core = up_j(1), c
         elif k == 2:
             j, core = h, 1 - c
-        elif k == 3:
-            j, core, size = up_j(2), c, HALF
-        elif k == 4:
-            j, core, lo, size = up_j(2), c, HALF, SENT - HALF
+        elif k in (3, 4):
+            j, core, half = up_j(2), c, k - 3
         elif k in (5, 6):
             j, core = up_j(3 if k == 5 else 1), 1 - c
-        elif k == 7:
-            j, core, size = up_j(2), 1 - c, HALF
         else:
-            j, core, lo, size = up_j(2), 1 - c, HALF, SENT - HALF
-        part = shard(a, w, j, core, lo, size)
+            j, core, half = up_j(2), 1 - c, k - 7
+        part = shard(a, w, j, core, half)
         return remote(part, part, s, r, me.sibling)
 
     for a in (3, 0, 1):
@@ -312,11 +324,18 @@
 
     def project(j, first):
         cols = pl.ds(mul(j * PAIR, 128), PAIR)
-        rest = wrem[cols, :].astype(F32)
-        lane = lax.broadcasted_iota(jnp.int32, (PAIR, 128), 1)
-        for a in range(3):
-            own = rest if a == 0 else pltpu.roll(rest, 128 - REST * a, 1)
-            weights[a][cols, MAIN:] = jnp.where(lane < REST, own, 0.0).astype(BF16)
+        live = lax.broadcasted_iota(jnp.int32, (SENT + 8, 128), 0) < OWN
+        live = live & (lax.broadcasted_iota(jnp.int32, (SENT + 8, 128), 1) < REST)
+        for core in range(2):
+            misc = wrem[misc_at(j, core), :].astype(F32)
+            rest = misc[: SENT + 8]
+            for a in range(3):
+                own = rest if a == 0 else pltpu.roll(rest, 128 - REST * a, 1)
+                weights[a][rows_at(j, core, 0, SENT + 8), MAIN:] = jnp.where(live, own, 0.0).astype(BF16)
+                for t in range(TILES):
+                    at = OWN + TAIL * (a * TILES + t)
+                    last = jnp.concatenate([misc[at : at + TAIL], jnp.zeros((8 - TAIL, 128), F32)], axis=0)
+                    weights[a][rows_at(j, core, SENT, 8), 128 * t : 128 * (t + 1)] = last.astype(BF16)
 
         @pl.loop(0, 2)
         def _(m):
@@ -370,8 +389,9 @@
             return (ra_d if a == 0 else ra_rem).at[k]
         return (recv_x, recv_g)[a - 1].at[pl.ds(CHUNK * k, SENT), width(a)]
 
-    def half_in(a, lo, size):
-        return hr.at[a, pl.ds(lo, size), :] if a < 3 else hr_rem.at[pl.ds(lo, size), :]
+    def half_in(a, k):
+        rows = pl.ds(*span(a, k))
+        return hr.at[a, rows, :] if a < 3 else hr_rem.at[rows, :]
 
     def full_in(a, k):
         return fr.at[a * 2 + k] if a < 3 else fr_rem.at[k]
@@ -388,18 +408,27 @@
             part = dot_tn(left[:, cols], right[...])
             parts[cols, :MAIN] = part[:, :MAIN].astype(BF16)
             exchange(a, k).start()
-            rest = part[:, MAIN:]
-            if a > 0:
-                rest = grem[cols, :].astype(F32) + pltpu.roll(rest, REST * a, 1)
-            grem[cols, :] = rest.astype(BF16)
+            for core in range(2):
+                own = part[CHUNK * core : CHUNK * core + OWN]
+                rest = own[:, MAIN:] if a == 0 else pltpu.roll(own[:, MAIN:], REST * a, 1)
+                pieces = [rest]
+                if a > 0:
+                    pieces.append(jnp.zeros((a * TILES * TAIL, 128), F32))
+                pieces += [own[SENT:, 128 * t : 128 * (t + 1)] for t in range(TILES)]
+                if a < 2:
+                    pieces.append(jnp.zeros(((2 - a) * TILES * TAIL, 128), F32))
+                misc = jnp.concatenate(pieces, axis=0)
+                at = misc_at(up_j(k), core)
+                if a > 0:
+                    misc = misc + grem[at, :].astype(F32)
+                grem[at, :] = misc.astype(BF16)
             if a == 2:
                 exchange(3, k).start()
 
     def half(a, k):
-        lo, size = ((0, HALF), (HALF, SENT - HALF))[k]
         return remote(
-            shard(a, arrays[a][0], up_j(2), c, lo, size),
-            half_in(a, lo, size),
+            shard(a, arrays[a][0], up_j(2), c, k),
+            half_in(a, k),
             hss.at[a * 2 + k],
             hsr.at[a * 2 + k],
             (me.up, me.down)[k],
@@ -416,7 +445,7 @@
 
     def send_halves(a):
         exchange(a, 2).wait_recv()
-        at = rows_at(up_j(2), c), width(a)
+        at = place_of(a, up_j(2), c)
         parts = arrays[a][0]
         parts[at] = (parts[at].astype(F32) + ra(a, 2)[...].astype(F32)).astype(BF16)
         half(a, 0).start()
@@ -428,11 +457,11 @@
             exchange(a, jj).wait_recv()
             half(a, k).wait_recv()
             for with_half in (True, False):
-                lo, size = ((0, HALF), (HALF, SENT - HALF))[k if with_half else 1 - k]
-                at = rows_at(up_j(jj), c, lo, size), width(a)
-                total = parts[at].astype(F32) + ra(a, jj)[lo : lo + size, :].astype(F32)
+                side = k if with_half else 1 - k
+                at = place_of(a, up_j(jj), c, side)
+                total = parts[at].astype(F32) + ra(a, jj)[pl.ds(*span(a, side)), :].astype(F32)
                 if with_half:
-                    total = total + half_in(a, lo, size)[...].astype(F32)
+                    total = total + half_in(a, k)[...].astype(F32)
                 parts[at] = total.astype(BF16)
             full(a, k).start()
 
@@ -466,8 +495,8 @@
     for a in (3, 0, 1):
         for k in range(9):
             ag(a, k).wait_send()
+    forward_neighbours(2)
     send_halves(0)
-    forward_neighbours(2)
     ag_in(2, 2).wait_recv()
     down_step(h, True)
     out_step(h)
@@ -475,7 +504,6 @@
     down_step(up_j(3), False)
     ag_in(2, 6).wait_recv()
     down_step(up_j(1), False)
-    send_fulls(0)
     finish_gather(2)
     wait_opposite(2)
     down_step(up_j(2), False)
@@ -489,6 +517,7 @@
 
     parts_of(1, (2, 1))
     send_halves(1)
+    send_fulls(0)
     parts_of(1, (3, 0))
     parts_of(2, (2, 1))
     send_halves(2)
@@ -548,20 +577,6 @@
         at = slice(OWN * k, OWN * (k + 1))
         mixed_out[at, :] = (own[CHUNK * k : CHUNK * k + OWN, :] + zrecv[at, :].astype(F32)).astype(BF16)
 
-    for a in range(4):
-        exchange(a, 0).wait_recv()
-        total = arrays[a][0][rows_at(h, c), width(a)].astype(F32) + ra(a, 0)[...].astype(F32)
-        for k in range(2):
-            full(a, k).wait_recv()
-            total = total + full_in(a, k)[...].astype(F32)
-        if a < 3:
-            outs[a][:, :MAIN] = total.astype(BF16)[:OWN]
-        else:
-            for b in range(3):
-                own = total if b == 0 else pltpu.roll(total, 128 - REST * b, 1)
-                outs[b][:, MAIN:] = own.astype(BF16)[:OWN, :REST]
-
-    zcopy.wait_send()
     for k in range(9):
         ag(2, k).wait_send()
     for a in range(4):
@@ -569,12 +584,32 @@
             exchange(a, k).wait_send()
         for k in range(2):
             half(a, k).wait_send()
-            full(a, k).wait_send()
     for bi in range(2):
 
         @pl.loop(1, 16)
         def _(i):
             back_copy(bi, i, False).wait_send()
+
+    for a in range(4):
+        exchange(a, 0).wait_recv()
+        total = arrays[a][0][place_of(a, h, c)].astype(F32) + ra(a, 0)[...].astype(F32)
+        for k in range(2):
+            full(a, k).wait_recv()
+            total = total + full_in(a, k)[...].astype(F32)
+        if a < 3:
+            outs[a][:SENT, :MAIN] = total.astype(BF16)
+        else:
+            for b in range(3):
+                own = total[:OWN] if b == 0 else pltpu.roll(total[:OWN], 128 - REST * b, 1)
+                outs[b][:, MAIN:] = own.astype(BF16)[:, :REST]
+                for t in range(TILES):
+                    at = OWN + TAIL * (b * TILES + t)
+                    outs[b][SENT:, 128 * t : 128 * (t + 1)] = total[at : at + TAIL].astype(BF16)
+
+    zcopy.wait_send()
+    for a in range(4):
+        for k in range(2):
+            full(a, k).wait_send()
 
 
 def copy_kernel(*refs):
@@ -603,8 +638,8 @@
         in_specs=[VM()] * 4 + [anywhere] * 3,
         out_specs=[VM()] * 4,
         scratch_shapes=[
-            b16(DP, DP), b16(DP, DP), b16(DP, DP), b16(DP, 128), b16(DP, 128),
-            b16(4, SENT, 128), b16(SENT, 128), b16(2, SENT, 128),
+            b16(DP, DP), b16(DP, DP), b16(DP, DP), b16(8 * MISC, 128), b16(8 * MISC, 128),
+            b16(4, MISC, 128), b16(MISC, 128), b16(2, MISC, 128),
             f32(8, TOK), f32(8, TOK), b16(DP, TOK), b16(DP, TOK), b16(D, TOK), b16(D, TOK),
             b16(SLOTS, DP), b16(SLOTS, DP), b16(SLOTS, DP), b16(SLOTS, DP),
             b16(CAP, DP), b16(CAP, DP), b16(CAP, DP), b16(CAP, DP),

time: 258 us -> 254 us (0.984)
  Pallas kernels: 256 us -> 250 us
    pallas_call x1, Pallas kernels: 253 us -> 247 us  [body(): pl.pallas_call(step_kernel, name='step', out_shape=results, in_specs=[VM(...]
where the time goes in v5:
time: 254 us; the launch traced here: 251 us
  Pallas kernels  250 us (98%)
    pallas_call x1, Pallas kernels, body(): pl.pallas_call(step_kernel, name='step', out_shape=results, in_specs=[VM(...  247 us

profile of v5, /device:TPU:56, one launch (start us, length us, event | category | flops | bytes accessed | tf_op | source)
XLA Modules:
  0.0 250.6 jit_solution(1704074732901144416)
XLA Ops:
  0.6 247.4 %step.1 = (bf16[180,1440]{1,0:T(8,128)(2,1)}, bf16[180,1440]{1,0:T(8,128)(2,1)}, bf16[180,1440]{1,0:T(8,128)(2,1)}, bf16[1440,128]{1,0:T(8,128)(2,1)}) custom-call(s32[4,128]{1,0:T(4,128)} %bitcast.10, f32[4,128]{1,0:T(4,128)} %bitcast.11, bf16[1440,128]{1,0:T(8,128)(2,1)} %bitcast.8, bf16[1440,128]{1,0:T(8,128)(2,1)} %bitcast.9, ...), custom_call_target="tpu_custom_call" | custom-call | tf_op jit(solution)/shard_map/step/pallas_call | solution.py:634
  248.0 2.4 results.1

commit v6 on v5

--- a/solution.py
+++ b/solution.py
@@ -103,9 +103,9 @@
 
 
 def step_kernel(
-    ids, gates_in, tok_in, cot_in, wg_in, wu_in, wd_in,
+    ids_hbm, gates_hbm, tok_hbm, cot_hbm, wg_in, wu_in, wd_in,
     gg_out, gu_out, gd_out, mixed_out,
-    wg, wu, wd, wrem, grem, ra_rem, hr_rem, fr_rem, meta, zmeta, tok, cot, ztok, zcot, send_x, send_g, recv_x, recv_g,
+    ids, gates_in, tok_in, cot_in, wg, wu, wd, wrem, grem, ra_rem, hr_rem, fr_rem, meta, zmeta, tok, cot, ztok, zcot, send_x, send_g, recv_x, recv_g,
     x, g, hid, eo, acc_g, acc_u, acc_d, pd, ra_d, hr, fr, rets, rr, r_mat, mt, zsend, zrecv,
     loc_sem, zs, zr, ags, agr, dss, dsr, d2s, d2r, hss, hsr, fss, fsr, rs, rr_sem,
 ):
@@ -149,6 +149,16 @@
     ]
     for cp in own_copies:
         cp.start()
+    inputs = [
+        pltpu.make_async_copy(src, dst, loc_sem.at[3 + k])
+        for k, (src, dst) in enumerate(
+            ((ids_hbm, ids), (gates_hbm, gates_in), (tok_hbm, tok_in), (cot_hbm, cot_in))
+        )
+    ]
+    for cp in inputs:
+        cp.start()
+    for cp in inputs[:2]:
+        cp.wait()
     meta[0:4, :] = ids[...].astype(F32)
     meta[4:8, :] = gates_in[...]
 
@@ -172,6 +182,8 @@
     ]
     wrem[misc_at(h, c), :] = jnp.concatenate([last_lanes, *last_rows], axis=0).astype(BF16)
 
+    for cp in inputs[2:]:
+        cp.wait()
     me.await_greetings()
 
     zex = [
@@ -517,11 +529,11 @@
 
     parts_of(1, (2, 1))
     send_halves(1)
-    send_fulls(0)
     parts_of(1, (3, 0))
     parts_of(2, (2, 1))
     send_halves(2)
     send_halves(3)
+    send_fulls(0)
     parts_of(2, (3, 0))
     for k in (3, 1, 2):
         out_step(up_j(k))
@@ -635,9 +647,10 @@
         step_kernel,
         name="step",
         out_shape=results,
-        in_specs=[VM()] * 4 + [anywhere] * 3,
+        in_specs=[anywhere] * 7,
         out_specs=[VM()] * 4,
         scratch_shapes=[
+            pltpu.VMEM((4, TOK), jnp.int32), f32(4, TOK), b16(D, TOK), b16(D, TOK),
             b16(DP, DP), b16(DP, DP), b16(DP, DP), b16(8 * MISC, 128), b16(8 * MISC, 128),
             b16(4, MISC, 128), b16(MISC, 128), b16(2, MISC, 128),
             f32(8, TOK), f32(8, TOK), b16(DP, TOK), b16(DP, TOK), b16(D, TOK), b16(D, TOK),
@@ -646,7 +659,7 @@
             f32(CAP, DP), f32(CAP, DP), f32(CAP, DP),
             b16(DP, DP), b16(4, SENT, MAIN), b16(3, SENT, MAIN), b16(6, SENT, MAIN),
             b16(SLOTS, DP), b16(SLOTS, DP), b16(CAP, SLOTS), f32(2, PLANE, TOK), b16(D, TOK), b16(D, TOK),
-            dma((3,)), dma((4,)), dma((4,)), dma((36,)), dma((36,)), dma((64,)), dma((64,)),
+            dma((7,)), dma((4,)), dma((4,)), dma((36,)), dma((36,)), dma((64,)), dma((64,)),
             dma((16,)), dma((16,)), dma((8,)), dma((8,)), dma((8,)), dma((8,)), dma((32,)), dma((32,)),
         ],
         compiler_params=pltpu.CompilerParams(

time: 254 us -> 248 us (0.976)
  Pallas kernels: 250 us -> 246 us
    pallas_call x1, Pallas kernels: 247 us -> 244 us  [body(): pl.pallas_call(step_kernel, name='step', out_shape=results, in_specs=[any...]
where the time goes in v6:
time: 248 us; the launch traced here: 247 us
  Pallas kernels  246 us (99%)
    pallas_call x1, Pallas kernels, body(): pl.pallas_call(step_kernel, name='step', out_shape=results, in_specs=[any...  244 us

profile of v6, /device:TPU:56, one launch (start us, length us, event | category | flops | bytes accessed | tf_op | source)
XLA Modules:
  0.0 247.0 jit_solution(3695182493396676024)
XLA Ops:
  0.6 243.7 %step.1 = (bf16[180,1440]{1,0:T(8,128)(2,1)}, bf16[180,1440]{1,0:T(8,128)(2,1)}, bf16[180,1440]{1,0:T(8,128)(2,1)}, bf16[1440,128]{1,0:T(8,128)(2,1)}) custom-call(s32[4,128]{1,0:T(4,128)} %bitcast.10, f32[4,128]{1,0:T(4,128)} %bitcast.11, bf16[1440,128]{1,0:T(8,128)(2,1)} %bitcast.8, bf16[1440,128]{1,0:T(8,128)(2,1)} %bitcast.9, ...), custom_call_target="tpu_custom_call" | custom-call | tf_op jit(solution)/shard_map/step/pallas_call | solution.py:646
  244.4 2.4 results.1

commit v7 on v6

--- a/solution.py
+++ b/solution.py
@@ -563,6 +563,9 @@
         def _(i):
             back_copy(bi, i, False).start()
 
+    send_fulls(2)
+    send_fulls(3)
+
     for bi in range(2):
 
         @pl.loop(1, 16)
@@ -581,8 +584,6 @@
         zsend[OWN * k : OWN * (k + 1), :] = theirs[CHUNK * k : CHUNK * k + OWN, :]
     zcopy = remote(zsend, zrecv, zs.at[3], zr.at[3], me.partner)
     zcopy.start()
-    send_fulls(2)
-    send_fulls(3)
     own = combine(0)
     zcopy.wait_recv()
     for k in range(8):

time: 248 us -> 250 us (level); the launches traced: 247 us -> 246 us
  no operation moved by 1% of the time
where the time goes in v7:
time: 250 us; the launch traced here: 246 us
  Pallas kernels  245 us (98%)
    pallas_call x1, Pallas kernels, body(): pl.pallas_call(step_kernel, name='step', out_shape=results, in_specs=[any...  243 us

profile of v7, /device:TPU:56, one launch (start us, length us, event | category | flops | bytes accessed | tf_op | source)
XLA Modules:
  0.0 245.8 jit_solution(8116415214602614434)
XLA Ops:
  0.6 242.6 %step.1 = (bf16[180,1440]{1,0:T(8,128)(2,1)}, bf16[180,1440]{1,0:T(8,128)(2,1)}, bf16[180,1440]{1,0:T(8,128)(2,1)}, bf16[1440,128]{1,0:T(8,128)(2,1)}) custom-call(s32[4,128]{1,0:T(4,128)} %bitcast.10, f32[4,128]{1,0:T(4,128)} %bitcast.11, bf16[1440,128]{1,0:T(8,128)(2,1)} %bitcast.8, bf16[1440,128]{1,0:T(8,128)(2,1)} %bitcast.9, ...), custom_call_target="tpu_custom_call" | custom-call | tf_op jit(solution)/shard_map/step/pallas_call | solution.py:647
  243.3 2.4 results.1
